TPU v7x, 8 devices: a whole 2x2x1 slice. The times are simulated.
8 devices in a mesh: pp: 4 (over z, y, x), dp: 2 (over core).
Axes of the slice: x: 2, y: 2, z: 1, core: 2. Of those that a mesh axis runs over, the one named last changes fastest.
Arguments:
- act_in: bfloat16 [6, 32, 128, 1024], P(None, 'dp')
- loss_seed: bfloat16 [6, 32, 128, 1024], P(None, 'dp')
- w_qkv: bfloat16 [4, 1024, 48, 64], P('pp', 'dp')
- w_proj: bfloat16 [4, 1024, 1024], P('pp', 'dp')
- w_up: bfloat16 [4, 1024, 4096], P('pp', 'dp')
- w_down: bfloat16 [4, 4096, 1024], P('pp', 'dp')
Outputs:
- output 1: float32 [4, 1024, 48, 64], P('pp', 'dp')
- output 2: float32 [4, 1024, 1024], P('pp', 'dp')
- output 3: float32 [4, 1024, 4096], P('pp', 'dp')
- output 4: float32 [4, 4096, 1024], P('pp', 'dp')
- output 5: bfloat16 [6, 32, 128, 1024], P(None, 'dp', 'pp')
All inputs are finite; a program needn't handle non-finite values.
Results may differ from a plain program's by a relative error of at most 0.02.
Values are sent between devices in bfloat16 or wider.
A program may use at most 1 GiB of HBM per device.

v0:
```python
import jax
import jax.numpy as jnp
from jax import lax
from jax.sharding import PartitionSpec as P

NORM_EPS = 1e-6


def rms_norm(hidden):
    return hidden * lax.rsqrt(jnp.mean(hidden * hidden, axis=-1, keepdims=True) + NORM_EPS)


def gelu_tanh(pre_act):
    return jax.nn.gelu(pre_act, approximate=True)


def attn_core(q_heads, k_heads, v_heads):
    seq_len = q_heads.shape[1]
    scores = jnp.einsum('bqnh,bknh->bnqk', q_heads, k_heads, preferred_element_type=jnp.float32) * (q_heads.shape[-1] ** -0.5)
    causal = jnp.arange(seq_len)[:, None] >= jnp.arange(seq_len)[None, :]
    prob_bf = jax.nn.softmax(jnp.where(causal, scores, -1e30), axis=-1).astype(jnp.bfloat16)
    return jnp.einsum('bnqk,bknh->bqnh', prob_bf, v_heads, preferred_element_type=jnp.float32).astype(jnp.bfloat16)


def layer_forward(hidden, w_qkv, w_proj, w_up, w_down):
    num_heads = w_qkv.shape[1] // 3
    hid_f32 = hidden.astype(jnp.float32)
    normed = rms_norm(hid_f32).astype(jnp.bfloat16)
    qkv_act = jnp.einsum('bsd,dnh->bsnh', normed, w_qkv, preferred_element_type=jnp.float32).astype(jnp.bfloat16)
    q_heads = qkv_act[:, :, :num_heads]
    k_heads = qkv_act[:, :, num_heads:2 * num_heads]
    v_heads = qkv_act[:, :, 2 * num_heads:]
    attn_flat = attn_core(q_heads, k_heads, v_heads).reshape(hidden.shape)
    mid_f32 = (hid_f32 + jnp.einsum('bse,ed->bsd', attn_flat, w_proj, preferred_element_type=jnp.float32)).astype(jnp.bfloat16).astype(jnp.float32)
    normed2 = rms_norm(mid_f32).astype(jnp.bfloat16)
    up_act = jnp.einsum('bsd,df->bsf', normed2, w_up, preferred_element_type=jnp.float32).astype(jnp.bfloat16)
    gelu_out = gelu_tanh(up_act.astype(jnp.float32)).astype(jnp.bfloat16)
    block_out = (mid_f32 + jnp.einsum('bsf,fd->bsd', gelu_out, w_down, preferred_element_type=jnp.float32)).astype(jnp.bfloat16)
    saved_acts = (hid_f32, normed, q_heads, k_heads, v_heads, attn_flat, mid_f32, normed2, up_act, gelu_out)
    return block_out, saved_acts


def layer_backward(saved_acts, ct_out, w_qkv, w_proj, w_up, w_down):
    hid_f32, normed, q_heads, k_heads, v_heads, attn_flat, mid_f32, normed2, up_act, gelu_out = saved_acts
    g_down = jnp.einsum('bsf,bsd->fd', gelu_out, ct_out, preferred_element_type=jnp.float32)
    ct_gelu = jnp.einsum('bsd,fd->bsf', ct_out, w_down, preferred_element_type=jnp.float32).astype(jnp.bfloat16)
    gelu_pull = jax.vjp(gelu_tanh, up_act.astype(jnp.float32))[1]
    ct_up = gelu_pull(ct_gelu.astype(jnp.float32))[0].astype(jnp.bfloat16)
    g_up = jnp.einsum('bsd,bsf->df', normed2, ct_up, preferred_element_type=jnp.float32)
    ct_norm2 = jnp.einsum('bsf,df->bsd', ct_up, w_up, preferred_element_type=jnp.float32).astype(jnp.bfloat16)
    norm_pull2 = jax.vjp(rms_norm, mid_f32)[1]
    ct_mid = (ct_out.astype(jnp.float32) + norm_pull2(ct_norm2.astype(jnp.float32))[0]).astype(jnp.bfloat16)
    g_proj = jnp.einsum('bse,bsd->ed', attn_flat, ct_mid, preferred_element_type=jnp.float32)
    ct_attn = jnp.einsum('bsd,ed->bse', ct_mid, w_proj, preferred_element_type=jnp.float32).astype(jnp.bfloat16)
    attn_pull = jax.vjp(attn_core, q_heads, k_heads, v_heads)[1]
    ct_q, ct_k, ct_v = attn_pull(ct_attn.reshape(q_heads.shape))
    ct_qkv = jnp.concatenate([ct_q, ct_k, ct_v], axis=2)
    g_qkv = jnp.einsum('bsd,bsnh->dnh', normed, ct_qkv, preferred_element_type=jnp.float32)
    ct_norm = jnp.einsum('bsnh,dnh->bsd', ct_qkv, w_qkv, preferred_element_type=jnp.float32).astype(jnp.bfloat16)
    norm_pull = jax.vjp(rms_norm, hid_f32)[1]
    ct_hidden = (ct_mid.astype(jnp.float32) + norm_pull(ct_norm.astype(jnp.float32))[0]).astype(jnp.bfloat16)
    return ct_hidden, (g_qkv, g_proj, g_up, g_down)


def stage_forward(hidden, weights):
    for layer_idx in range(weights[0].shape[0]):
        hidden = layer_forward(hidden, weights[0][layer_idx], weights[1][layer_idx], weights[2][layer_idx], weights[3][layer_idx])[0]
    return hidden


def stage_backward(hidden, ct_out, weights):
    num_layers = weights[0].shape[0]
    saved_list = []
    for layer_idx in range(num_layers):
        layer_w = tuple(w_full[layer_idx] for w_full in weights)
        hidden, saved_acts = layer_forward(hidden, *layer_w)
        saved_list.append(saved_acts)
    grad_lists = ([], [], [], [])
    for layer_idx in reversed(range(num_layers)):
        layer_w = tuple(w_full[layer_idx] for w_full in weights)
        ct_out, layer_grads = layer_backward(saved_list[layer_idx], ct_out, *layer_w)
        for grad_list, grad_part in zip(grad_lists, layer_grads):
            grad_list.append(grad_part)
    return ct_out, tuple(jnp.stack(grad_list[::-1]) for grad_list in grad_lists)


def solution(mesh):
    stages = mesh.shape['pp']
    fwd_pairs = [(src_idx, src_idx + 1) for src_idx in range(stages - 1)]
    bwd_pairs = [(src_idx + 1, src_idx) for src_idx in range(stages - 1)]

    def device_step(act_in, loss_seed, w_qkv, w_proj, w_up, w_down):
        num_micro = act_in.shape[0]
        num_ticks = num_micro + 2 * stages - 2
        stage_idx = lax.axis_index('pp')
        weights = tuple(lax.all_gather(w_part, 'dp', axis=1, tiled=True) for w_part in (w_qkv, w_proj, w_up, w_down))
        zero_act = jnp.zeros(act_in.shape[1:], jnp.bfloat16)
        grad_init = tuple(jnp.zeros(w_full.shape, jnp.float32) for w_full in weights)

        def run_forward(hidden):
            return stage_forward(hidden, weights)

        def run_backward(hidden, ct_out, grad_acc):
            ct_in, stage_grads = stage_backward(hidden, ct_out, weights)
            return ct_in, tuple(acc_part + grad_part for acc_part, grad_part in zip(grad_acc, stage_grads))

        def skip_backward(hidden, ct_out, grad_acc):
            return jnp.zeros_like(hidden), grad_acc

        def run_tick(tick_idx, loop_state):
            fwd_buf, bwd_buf, stash_in, outputs, grad_acc = loop_state
            fwd_idx = tick_idx - stage_idx
            fwd_ok = (fwd_idx >= 0) & (fwd_idx < num_micro)
            fwd_slot = jnp.clip(fwd_idx, 0, num_micro - 1)
            fresh_in = lax.dynamic_index_in_dim(act_in, fwd_slot, 0, keepdims=False)
            stage_in = jnp.where(stage_idx == 0, fresh_in, fwd_buf)
            stage_out = lax.cond(fwd_ok, run_forward, jnp.zeros_like, stage_in)
            old_in = lax.dynamic_index_in_dim(stash_in, fwd_slot, 0, keepdims=False)
            stash_in = lax.dynamic_update_index_in_dim(stash_in, jnp.where(fwd_ok, stage_in, old_in), fwd_slot, 0)
            old_out = lax.dynamic_index_in_dim(outputs, fwd_slot, 0, keepdims=False)
            outputs = lax.dynamic_update_index_in_dim(outputs, jnp.where(fwd_ok, stage_out, old_out), fwd_slot, 0)
            bwd_idx = tick_idx - (2 * stages - 2) + stage_idx
            bwd_ok = (bwd_idx >= 0) & (bwd_idx < num_micro)
            bwd_slot = jnp.clip(bwd_idx, 0, num_micro - 1)
            seed_now = lax.dynamic_index_in_dim(loss_seed, bwd_slot, 0, keepdims=False)
            ct_out = jnp.where(stage_idx == stages - 1, seed_now, bwd_buf)
            saved_in = lax.dynamic_index_in_dim(stash_in, bwd_slot, 0, keepdims=False)
            ct_in, grad_acc = lax.cond(bwd_ok, run_backward, skip_backward, saved_in, ct_out, grad_acc)
            fwd_buf = lax.ppermute(stage_out, 'pp', fwd_pairs)
            bwd_buf = lax.ppermute(ct_in, 'pp', bwd_pairs)
            return fwd_buf, bwd_buf, stash_in, outputs, grad_acc

        loop_init = (zero_act, zero_act, jnp.zeros_like(act_in), jnp.zeros_like(act_in), grad_init)
        loop_state = lax.fori_loop(0, num_ticks, run_tick, loop_init)
        outputs, grad_acc = loop_state[3], loop_state[4]
        grad_shards = tuple(lax.psum_scatter(acc_part, 'dp', scatter_dimension=1, tiled=True) for acc_part in grad_acc)
        last_out = jnp.where(stage_idx == stages - 1, outputs, jnp.zeros_like(outputs))
        out_shard = lax.psum_scatter(last_out, 'pp', scatter_dimension=2, tiled=True)
        return grad_shards + (out_shard,)

    weight_spec = P('pp', 'dp')
    act_spec = P(None, 'dp')
    return jax.shard_map(device_step, mesh=mesh, in_specs=(act_spec, act_spec, weight_spec, weight_spec, weight_spec, weight_spec), out_specs=(weight_spec, weight_spec, weight_spec, weight_spec, P(None, 'dp', 'pp')), check_vma=False)
```

profile of v0, /device:TPU:0, one launch (start us, length us, event | category | flops | bytes accessed | tf_op | source)
XLA Modules:
  0.0 6166.1 jit_solution(15091815812836028415)
XLA Ops:
  125.4 5734.2 %while.29 = (s32[]{:T(128)}, bf16[16,128,1024]{2,1,0:T(8,128)(2,1)}, bf16[16,128,1024]{2,1,0:T(8,128)(2,1)}, bf16[6,16,128,1024]{3,2,1,0:T(8,128)(2,1)}, bf16[6,...) while((s32[]{:T(128)}, ...), condition=%wide.region_16.17_spmd, body=%wide.region_0.16_spmd.sunk | while | flops 194026536960 | bytes 1134478848 | solution.py:134
  134.9 122.1 %conditional.4 = (bf16[16,128,1024]{2,1,0:T(8,128)(2,1)}) conditional(s32[]{:T(128)} %convert_element_type.489, () %tuple.76, (bf16[16,128,1024]{2,1,0:T(8,128)(2,1)}, bf16[1,1024,48,64]{1,3,2,0:T(8,128)(2,1)}, bf16[1,1024,1024]{2,1,0:T(8,128)(2,1)S(1)}, bf16[1,1024,4096]{2,1,0:T(8,128)(2,1)}, bf16[1,4096,1024]{2,1,0:T(8,128)(2,1)}) %tuple.77), branch_computations={%region_1.1_spmd, %region_2.6_spmd} | conditional | flops 52785336320 | bytes 222658592 | solution.py:117
  202.4 30.0 fusion.172
  274.6 74.1 %collective-permute-done = bf16[16,128,1024]{2,1,0:T(8,128)(2,1)} collective-permute-done((bf16[16,128,1024]{2,1,0:T(8,128)(2,1)}, bf16[16,128,1024]{2,1,0:T(8,128)(2,1)}, u32[]{:S(2)}, u32[]{:S(2)}) %collective-permute-start) | collective-permute-done | bytes 4194336 | tf_op jit(solution)/shard_map/while/body/eval_jaxpr/ppermute | solution.py:129
  370.3 122.0 %conditional.4 = (bf16[16,128,1024]{2,1,0:T(8,128)(2,1)}) conditional(s32[]{:T(128)} %convert_element_type.489, () %tuple.76, (bf16[16,128,1024]{2,1,0:T(8,128)(2,1)}, bf16[1,1024,48,64]{1,3,2,0:T(8,128)(2,1)}, bf16[1,1024,1024]{2,1,0:T(8,128)(2,1)S(1)}, bf16[1,1024,4096]{2,1,0:T(8,128)(2,1)}, bf16[1,4096,1024]{2,1,0:T(8,128)(2,1)}) %tuple.77), branch_computations={%region_1.1_spmd, %region_2.6_spmd} | conditional | flops 52785336320 | bytes 222658592 | solution.py:117
  437.8 30.0 fusion.172
  510.7 73.0 %collective-permute-done = bf16[16,128,1024]{2,1,0:T(8,128)(2,1)} collective-permute-done((bf16[16,128,1024]{2,1,0:T(8,128)(2,1)}, bf16[16,128,1024]{2,1,0:T(8,128)(2,1)}, u32[]{:S(2)}, u32[]{:S(2)}) %collective-permute-start) | collective-permute-done | bytes 4194336 | tf_op jit(solution)/shard_map/while/body/eval_jaxpr/ppermute | solution.py:129
  583.7 90.7 %collective-permute-done.1 = bf16[16,128,1024]{2,1,0:T(8,128)(2,1)} collective-permute-done((bf16[16,128,1024]{2,1,0:T(8,128)(2,1)}, bf16[16,128,1024]{2,1,0:T(8,128)(2,1)}, u32[]{:S(2)}, u32[]{:S(2)}) %collective-permute-start.1) | collective-permute-done | bytes 4194336 | tf_op jit(solution)/shard_map/while/body/eval_jaxpr/ppermute | solution.py:130
  684.4 122.0 %conditional.4 = (bf16[16,128,1024]{2,1,0:T(8,128)(2,1)}) conditional(s32[]{:T(128)} %convert_element_type.489, () %tuple.76, (bf16[16,128,1024]{2,1,0:T(8,128)(2,1)}, bf16[1,1024,48,64]{1,3,2,0:T(8,128)(2,1)}, bf16[1,1024,1024]{2,1,0:T(8,128)(2,1)S(1)}, bf16[1,1024,4096]{2,1,0:T(8,128)(2,1)}, bf16[1,4096,1024]{2,1,0:T(8,128)(2,1)}) %tuple.77), branch_computations={%region_1.1_spmd, %region_2.6_spmd} | conditional | flops 52785336320 | bytes 222658592 | solution.py:117
  751.9 30.0 fusion.172
  825.0 72.3 %collective-permute-done = bf16[16,128,1024]{2,1,0:T(8,128)(2,1)} collective-permute-done((bf16[16,128,1024]{2,1,0:T(8,128)(2,1)}, bf16[16,128,1024]{2,1,0:T(8,128)(2,1)}, u32[]{:S(2)}, u32[]{:S(2)}) %collective-permute-start) | collective-permute-done | bytes 4194336 | tf_op jit(solution)/shard_map/while/body/eval_jaxpr/ppermute | solution.py:129
  897.3 90.7 %collective-permute-done.1 = bf16[16,128,1024]{2,1,0:T(8,128)(2,1)} collective-permute-done((bf16[16,128,1024]{2,1,0:T(8,128)(2,1)}, bf16[16,128,1024]{2,1,0:T(8,128)(2,1)}, u32[]{:S(2)}, u32[]{:S(2)}) %collective-permute-start.1) | collective-permute-done | bytes 4194336 | tf_op jit(solution)/shard_map/while/body/eval_jaxpr/ppermute | solution.py:130
  998.0 122.0 %conditional.4 = (bf16[16,128,1024]{2,1,0:T(8,128)(2,1)}) conditional(s32[]{:T(128)} %convert_element_type.489, () %tuple.76, (bf16[16,128,1024]{2,1,0:T(8,128)(2,1)}, bf16[1,1024,48,64]{1,3,2,0:T(8,128)(2,1)}, bf16[1,1024,1024]{2,1,0:T(8,128)(2,1)S(1)}, bf16[1,1024,4096]{2,1,0:T(8,128)(2,1)}, bf16[1,4096,1024]{2,1,0:T(8,128)(2,1)}) %tuple.77), branch_computations={%region_1.1_spmd, %region_2.6_spmd} | conditional | flops 52785336320 | bytes 222658592 | solution.py:117
  1065.5 30.0 fusion.172
  1138.5 71.8 %collective-permute-done = bf16[16,128,1024]{2,1,0:T(8,128)(2,1)} collective-permute-done((bf16[16,128,1024]{2,1,0:T(8,128)(2,1)}, bf16[16,128,1024]{2,1,0:T(8,128)(2,1)}, u32[]{:S(2)}, u32[]{:S(2)}) %collective-permute-start) | collective-permute-done | bytes 4194336 | tf_op jit(solution)/shard_map/while/body/eval_jaxpr/ppermute | solution.py:129
  1210.2 90.7 %collective-permute-done.1 = bf16[16,128,1024]{2,1,0:T(8,128)(2,1)} collective-permute-done((bf16[16,128,1024]{2,1,0:T(8,128)(2,1)}, bf16[16,128,1024]{2,1,0:T(8,128)(2,1)}, u32[]{:S(2)}, u32[]{:S(2)}) %collective-permute-start.1) | collective-permute-done | bytes 4194336 | tf_op jit(solution)/shard_map/while/body/eval_jaxpr/ppermute | solution.py:130
  1310.9 122.0 %conditional.4 = (bf16[16,128,1024]{2,1,0:T(8,128)(2,1)}) conditional(s32[]{:T(128)} %convert_element_type.489, () %tuple.76, (bf16[16,128,1024]{2,1,0:T(8,128)(2,1)}, bf16[1,1024,48,64]{1,3,2,0:T(8,128)(2,1)}, bf16[1,1024,1024]{2,1,0:T(8,128)(2,1)S(1)}, bf16[1,1024,4096]{2,1,0:T(8,128)(2,1)}, bf16[1,4096,1024]{2,1,0:T(8,128)(2,1)}) %tuple.77), branch_computations={%region_1.1_spmd, %region_2.6_spmd} | conditional | flops 52785336320 | bytes 222658592 | solution.py:117
  1378.4 30.0 fusion.172
  1451.3 71.2 %collective-permute-done = bf16[16,128,1024]{2,1,0:T(8,128)(2,1)} collective-permute-done((bf16[16,128,1024]{2,1,0:T(8,128)(2,1)}, bf16[16,128,1024]{2,1,0:T(8,128)(2,1)}, u32[]{:S(2)}, u32[]{:S(2)}) %collective-permute-start) | collective-permute-done | bytes 4194336 | tf_op jit(solution)/shard_map/while/body/eval_jaxpr/ppermute | solution.py:129
  1522.6 212.9 %collective-permute-done.1 = bf16[16,128,1024]{2,1,0:T(8,128)(2,1)} collective-permute-done((bf16[16,128,1024]{2,1,0:T(8,128)(2,1)}, bf16[16,128,1024]{2,1,0:T(8,128)(2,1)}, u32[]{:S(2)}, u32[]{:S(2)}) %collective-permute-start.1) | collective-permute-done | bytes 4194336 | tf_op jit(solution)/shard_map/while/body/eval_jaxpr/ppermute | solution.py:130
  1745.5 122.1 %conditional.4 = (bf16[16,128,1024]{2,1,0:T(8,128)(2,1)}) conditional(s32[]{:T(128)} %convert_element_type.489, () %tuple.76, (bf16[16,128,1024]{2,1,0:T(8,128)(2,1)}, bf16[1,1024,48,64]{1,3,2,0:T(8,128)(2,1)}, bf16[1,1024,1024]{2,1,0:T(8,128)(2,1)S(1)}, bf16[1,1024,4096]{2,1,0:T(8,128)(2,1)}, bf16[1,4096,1024]{2,1,0:T(8,128)(2,1)}) %tuple.77), branch_computations={%region_1.1_spmd, %region_2.6_spmd} | conditional | flops 52785336320 | bytes 222658592 | solution.py:117
  1813.0 30.0 fusion.172
  1867.6 289.7 %collective-permute-start = (bf16[16,128,1024]{2,1,0:T(8,128)(2,1)}, bf16[16,128,1024]{2,1,0:T(8,128)(2,1)}, u32[]{:S(2)}, u32[]{:S(2)}) collective-permute-start(bf16[16,128,1024]{2,1,0:T(8,128)(2,1)} %get-tuple-element.824), channel_id=1, source_target_pairs={{0,2},{2,4},{4,6},{1,3},{3,5},{5,7}} | collective-permute-start | bytes 12582920 | tf_op jit(solution)/shard_map/while/body/eval_jaxpr/ppermute | solution.py:129
  2171.7 69.9 %collective-permute-done = bf16[16,128,1024]{2,1,0:T(8,128)(2,1)} collective-permute-done((bf16[16,128,1024]{2,1,0:T(8,128)(2,1)}, bf16[16,128,1024]{2,1,0:T(8,128)(2,1)}, u32[]{:S(2)}, u32[]{:S(2)}) %collective-permute-start) | collective-permute-done | bytes 4194336 | tf_op jit(solution)/shard_map/while/body/eval_jaxpr/ppermute | solution.py:129
  2241.6 376.5 %collective-permute-done.1 = bf16[16,128,1024]{2,1,0:T(8,128)(2,1)} collective-permute-done((bf16[16,128,1024]{2,1,0:T(8,128)(2,1)}, bf16[16,128,1024]{2,1,0:T(8,128)(2,1)}, u32[]{:S(2)}, u32[]{:S(2)}) %collective-permute-start.1) | collective-permute-done | bytes 4194336 | tf_op jit(solution)/shard_map/while/body/eval_jaxpr/ppermute | solution.py:130
  2640.4 117.1 %collective-permute-start = (bf16[16,128,1024]{2,1,0:T(8,128)(2,1)}, bf16[16,128,1024]{2,1,0:T(8,128)(2,1)}, u32[]{:S(2)}, u32[]{:S(2)}) collective-permute-start(bf16[16,128,1024]{2,1,0:T(8,128)(2,1)} %get-tuple-element.824), channel_id=1, source_target_pairs={{0,2},{2,4},{4,6},{1,3},{3,5},{5,7}} | collective-permute-start | bytes 12582920 | tf_op jit(solution)/shard_map/while/body/eval_jaxpr/ppermute | solution.py:129
  2757.5 372.5 %conditional.5 = (bf16[16,128,1024]{2,1,0:T(8,128)(2,1)}, f32[1,1024,48,64]{1,3,2,0:T(8,128)}, f32[1,1024,1024]{2,1,0:T(8,128)}, f32[1,1024,4096]{2,1,0:T(8,128)}, f32[1,4096,1024]{2,1,0:T(8,128)}) conditional(s32[]{:T(128)} %convert_element_type.490, (f32[1,1024,48,64]{1,3,2,0:T(8,128)}, f32[1,1024,1024]{2,1,0:T(8,128)}, ...), branch_computations={%region_7.7_spmd, %region_8.15_spmd} | conditional | flops 141234913280 | bytes 802767360 | solution.py:128
  2846.3 25.2 convolution_convert_fusion.1
  2871.5 43.6 fusion.55
  2939.1 28.7 bitcast_add_fusion.1
  2974.4 34.5 bitcast_add_fusion
  3139.0 80.0 %collective-permute-done.1 = bf16[16,128,1024]{2,1,0:T(8,128)(2,1)} collective-permute-done((bf16[16,128,1024]{2,1,0:T(8,128)(2,1)}, bf16[16,128,1024]{2,1,0:T(8,128)(2,1)}, u32[]{:S(2)}, u32[]{:S(2)}) %collective-permute-start.1) | collective-permute-done | bytes 4194336 | tf_op jit(solution)/shard_map/while/body/eval_jaxpr/ppermute | solution.py:130
  3245.3 372.5 %conditional.5 = (bf16[16,128,1024]{2,1,0:T(8,128)(2,1)}, f32[1,1024,48,64]{1,3,2,0:T(8,128)}, f32[1,1024,1024]{2,1,0:T(8,128)}, f32[1,1024,4096]{2,1,0:T(8,128)}, f32[1,4096,1024]{2,1,0:T(8,128)}) conditional(s32[]{:T(128)} %convert_element_type.490, (f32[1,1024,48,64]{1,3,2,0:T(8,128)}, f32[1,1024,1024]{2,1,0:T(8,128)}, ...), branch_computations={%region_7.7_spmd, %region_8.15_spmd} | conditional | flops 141234913280 | bytes 802767360 | solution.py:128
  3334.1 25.2 convolution_convert_fusion.1
  3359.3 43.6 fusion.55
  3426.9 28.7 bitcast_add_fusion.1
  3462.2 34.5 bitcast_add_fusion
  3626.8 184.6 %collective-permute-done.1 = bf16[16,128,1024]{2,1,0:T(8,128)(2,1)} collective-permute-done((bf16[16,128,1024]{2,1,0:T(8,128)(2,1)}, bf16[16,128,1024]{2,1,0:T(8,128)(2,1)}, u32[]{:S(2)}, u32[]{:S(2)}) %collective-permute-start.1) | collective-permute-done | bytes 4194336 | tf_op jit(solution)/shard_map/while/body/eval_jaxpr/ppermute | solution.py:130
  3841.0 372.5 %conditional.5 = (bf16[16,128,1024]{2,1,0:T(8,128)(2,1)}, f32[1,1024,48,64]{1,3,2,0:T(8,128)}, f32[1,1024,1024]{2,1,0:T(8,128)}, f32[1,1024,4096]{2,1,0:T(8,128)}, f32[1,4096,1024]{2,1,0:T(8,128)}) conditional(s32[]{:T(128)} %convert_element_type.490, (f32[1,1024,48,64]{1,3,2,0:T(8,128)}, f32[1,1024,1024]{2,1,0:T(8,128)}, ...), branch_computations={%region_7.7_spmd, %region_8.15_spmd} | conditional | flops 141234913280 | bytes 802767360 | solution.py:128
  3929.8 25.2 convolution_convert_fusion.1
  3955.0 43.6 fusion.55
  4022.6 28.7 bitcast_add_fusion.1
  4057.9 34.5 bitcast_add_fusion
  4222.5 77.6 %collective-permute-done.1 = bf16[16,128,1024]{2,1,0:T(8,128)(2,1)} collective-permute-done((bf16[16,128,1024]{2,1,0:T(8,128)(2,1)}, bf16[16,128,1024]{2,1,0:T(8,128)(2,1)}, u32[]{:S(2)}, u32[]{:S(2)}) %collective-permute-start.1) | collective-permute-done | bytes 4194336 | tf_op jit(solution)/shard_map/while/body/eval_jaxpr/ppermute | solution.py:130
  4322.4 110.0 %collective-permute-start = (bf16[16,128,1024]{2,1,0:T(8,128)(2,1)}, bf16[16,128,1024]{2,1,0:T(8,128)(2,1)}, u32[]{:S(2)}, u32[]{:S(2)}) collective-permute-start(bf16[16,128,1024]{2,1,0:T(8,128)(2,1)} %get-tuple-element.824), channel_id=1, source_target_pairs={{0,2},{2,4},{4,6},{1,3},{3,5},{5,7}} | collective-permute-start | bytes 12582920 | tf_op jit(solution)/shard_map/while/body/eval_jaxpr/ppermute | solution.py:129
  4432.4 372.5 %conditional.5 = (bf16[16,128,1024]{2,1,0:T(8,128)(2,1)}, f32[1,1024,48,64]{1,3,2,0:T(8,128)}, f32[1,1024,1024]{2,1,0:T(8,128)}, f32[1,1024,4096]{2,1,0:T(8,128)}, f32[1,4096,1024]{2,1,0:T(8,128)}) conditional(s32[]{:T(128)} %convert_element_type.490, (f32[1,1024,48,64]{1,3,2,0:T(8,128)}, f32[1,1024,1024]{2,1,0:T(8,128)}, ...), branch_computations={%region_7.7_spmd, %region_8.15_spmd} | conditional | flops 141234913280 | bytes 802767360 | solution.py:128
  4546.4 43.6 fusion.55
  4614.0 28.7 bitcast_add_fusion.1
  4649.4 34.5 bitcast_add_fusion
  4813.9 77.0 %collective-permute-done.1 = bf16[16,128,1024]{2,1,0:T(8,128)(2,1)} collective-permute-done((bf16[16,128,1024]{2,1,0:T(8,128)(2,1)}, bf16[16,128,1024]{2,1,0:T(8,128)(2,1)}, u32[]{:S(2)}, u32[]{:S(2)}) %collective-permute-start.1) | collective-permute-done | bytes 4194336 | tf_op jit(solution)/shard_map/while/body/eval_jaxpr/ppermute | solution.py:130
  4918.4 372.5 %conditional.5 = (bf16[16,128,1024]{2,1,0:T(8,128)(2,1)}, f32[1,1024,48,64]{1,3,2,0:T(8,128)}, f32[1,1024,1024]{2,1,0:T(8,128)}, f32[1,1024,4096]{2,1,0:T(8,128)}, f32[1,4096,1024]{2,1,0:T(8,128)}) conditional(s32[]{:T(128)} %convert_element_type.490, (f32[1,1024,48,64]{1,3,2,0:T(8,128)}, f32[1,1024,1024]{2,1,0:T(8,128)}, ...), branch_computations={%region_7.7_spmd, %region_8.15_spmd} | conditional | flops 141234913280 | bytes 802767360 | solution.py:128
  5032.4 43.6 fusion.55
  5100.0 28.7 bitcast_add_fusion.1
  5135.3 34.5 bitcast_add_fusion
  5299.9 75.7 %collective-permute-done.1 = bf16[16,128,1024]{2,1,0:T(8,128)(2,1)} collective-permute-done((bf16[16,128,1024]{2,1,0:T(8,128)(2,1)}, bf16[16,128,1024]{2,1,0:T(8,128)(2,1)}, u32[]{:S(2)}, u32[]{:S(2)}) %collective-permute-start.1) | collective-permute-done | bytes 4194336 | tf_op jit(solution)/shard_map/while/body/eval_jaxpr/ppermute | solution.py:130
  5402.0 372.5 %conditional.5 = (bf16[16,128,1024]{2,1,0:T(8,128)(2,1)}, f32[1,1024,48,64]{1,3,2,0:T(8,128)}, f32[1,1024,1024]{2,1,0:T(8,128)}, f32[1,1024,4096]{2,1,0:T(8,128)}, f32[1,4096,1024]{2,1,0:T(8,128)}) conditional(s32[]{:T(128)} %convert_element_type.490, (f32[1,1024,48,64]{1,3,2,0:T(8,128)}, f32[1,1024,1024]{2,1,0:T(8,128)}, ...), branch_computations={%region_7.7_spmd, %region_8.15_spmd} | conditional | flops 141234913280 | bytes 802767360 | solution.py:128
  5490.7 25.2 convolution_convert_fusion.1
  5515.9 43.6 fusion.55
  5583.5 28.7 bitcast_add_fusion.1
  5618.9 34.5 bitcast_add_fusion
  5783.4 74.7 %collective-permute-done.1 = bf16[16,128,1024]{2,1,0:T(8,128)(2,1)} collective-permute-done((bf16[16,128,1024]{2,1,0:T(8,128)(2,1)}, bf16[16,128,1024]{2,1,0:T(8,128)(2,1)}, u32[]{:S(2)}, u32[]{:S(2)}) %collective-permute-start.1) | collective-permute-done | bytes 4194336 | tf_op jit(solution)/shard_map/while/body/eval_jaxpr/ppermute | solution.py:130
  5886.9 25.8 reduce-scatter.10.cloned.1.call-done
  5912.7 25.8 reduce-scatter.12.cloned.1.call-done
  5938.5 220.7 %reduce-scatter.14.cloned.1.call-done = bf16[6,16,32,1024]{3,2,1,0:T(8,128)(2,1)} async-done(((bf16[6,16,128,1024]{3,2,1,0:T(8,128)(2,1)}), bf16[6,16,32,1024]{3,2,1,0:T(8,128)(2,1)}) %reduce-scatter.14.cloned.1.call-update) | async-done | bytes 6291472 | tf_op jit(solution)/shard_map/reduce_scatter | solution.py:138
  (701 shorter events, 2597.6 us)
Async XLA Ops:
  7.2 13.0 all-gather.7.cloned.1.call-start
  7.9 29.6 all-gather.5.cloned.1.call-start
  8.6 49.6 all-gather.9.cloned.1.call-start
  9.4 69.5 %all-gather.11.cloned.1.call-start = ((), (), s32[]{:S(2)}) async-start(), calls=%async_computation.8 | async-start | bytes 12582912 | tf_op jit(solution)/shard_map/all_gather | solution.py:96
  10.0 5861.4 %reduce-scatter.8.cloned.1.call-start = ((), (), s32[]{:S(2)}) async-start(), calls=%async_computation.10 | async-start | bytes 6291456 | tf_op jit(solution)/shard_map/reduce_scatter | solution.py:136
  257.0 91.7 %collective-permute-start = (bf16[16,128,1024]{2,1,0:T(8,128)(2,1)}, bf16[16,128,1024]{2,1,0:T(8,128)(2,1)}, u32[]{:S(2)}, u32[]{:S(2)}) collective-permute-start(bf16[16,128,1024]{2,1,0:T(8,128)(2,1)} %get-tuple-element.824), channel_id=1, source_target_pairs={{0,2},{2,4},{4,6},{1,3},{3,5},{5,7}} | collective-permute-start | bytes 12582920 | tf_op jit(solution)/shard_map/while/body/eval_jaxpr/ppermute | solution.py:129
  265.6 94.6 %collective-permute-start.1 = (bf16[16,128,1024]{2,1,0:T(8,128)(2,1)}, bf16[16,128,1024]{2,1,0:T(8,128)(2,1)}, u32[]{:S(2)}, u32[]{:S(2)}) collective-permute-start(bf16[16,128,1024]{2,1,0:T(8,128)(2,1)} %get-tuple-element.740), channel_id=1, source_target_pairs={{2,0},{4,2},{6,4},{3,1},{5,3},{7,5}} | collective-permute-start | bytes 12582920 | tf_op jit(solution)/shard_map/while/body/eval_jaxpr/ppermute | solution.py:130
  270.4 89.8 %copy-start.22 = (bf16[1,1024,1024]{2,1,0:T(8,128)(2,1)S(1)}, bf16[1,1024,1024]{2,1,0:T(8,128)(2,1)}, u32[]{:S(2)}) copy-start(bf16[1,1024,1024]{2,1,0:T(8,128)(2,1)} %get-tuple-element.884) | copy-start | bytes 6291460 | tf_op jit(solution)/shard_map/while
  492.3 91.3 %collective-permute-start = (bf16[16,128,1024]{2,1,0:T(8,128)(2,1)}, bf16[16,128,1024]{2,1,0:T(8,128)(2,1)}, u32[]{:S(2)}, u32[]{:S(2)}) collective-permute-start(bf16[16,128,1024]{2,1,0:T(8,128)(2,1)} %get-tuple-element.824), channel_id=1, source_target_pairs={{0,2},{2,4},{4,6},{1,3},{3,5},{5,7}} | collective-permute-start | bytes 12582920 | tf_op jit(solution)/shard_map/while/body/eval_jaxpr/ppermute | solution.py:129
  501.7 172.7 %collective-permute-start.1 = (bf16[16,128,1024]{2,1,0:T(8,128)(2,1)}, bf16[16,128,1024]{2,1,0:T(8,128)(2,1)}, u32[]{:S(2)}, u32[]{:S(2)}) collective-permute-start(bf16[16,128,1024]{2,1,0:T(8,128)(2,1)} %get-tuple-element.740), channel_id=1, source_target_pairs={{2,0},{4,2},{6,4},{3,1},{5,3},{7,5}} | collective-permute-start | bytes 12582920 | tf_op jit(solution)/shard_map/while/body/eval_jaxpr/ppermute | solution.py:130
  506.4 167.9 %copy-start.22 = (bf16[1,1024,1024]{2,1,0:T(8,128)(2,1)S(1)}, bf16[1,1024,1024]{2,1,0:T(8,128)(2,1)}, u32[]{:S(2)}) copy-start(bf16[1,1024,1024]{2,1,0:T(8,128)(2,1)} %get-tuple-element.884) | copy-start | bytes 6291460 | tf_op jit(solution)/shard_map/while
  806.4 90.9 %collective-permute-start = (bf16[16,128,1024]{2,1,0:T(8,128)(2,1)}, bf16[16,128,1024]{2,1,0:T(8,128)(2,1)}, u32[]{:S(2)}, u32[]{:S(2)}) collective-permute-start(bf16[16,128,1024]{2,1,0:T(8,128)(2,1)} %get-tuple-element.824), channel_id=1, source_target_pairs={{0,2},{2,4},{4,6},{1,3},{3,5},{5,7}} | collective-permute-start | bytes 12582920 | tf_op jit(solution)/shard_map/while/body/eval_jaxpr/ppermute | solution.py:129
  815.9 172.1 %collective-permute-start.1 = (bf16[16,128,1024]{2,1,0:T(8,128)(2,1)}, bf16[16,128,1024]{2,1,0:T(8,128)(2,1)}, u32[]{:S(2)}, u32[]{:S(2)}) collective-permute-start(bf16[16,128,1024]{2,1,0:T(8,128)(2,1)} %get-tuple-element.740), channel_id=1, source_target_pairs={{2,0},{4,2},{6,4},{3,1},{5,3},{7,5}} | collective-permute-start | bytes 12582920 | tf_op jit(solution)/shard_map/while/body/eval_jaxpr/ppermute | solution.py:130
  820.6 167.3 %copy-start.22 = (bf16[1,1024,1024]{2,1,0:T(8,128)(2,1)S(1)}, bf16[1,1024,1024]{2,1,0:T(8,128)(2,1)}, u32[]{:S(2)}) copy-start(bf16[1,1024,1024]{2,1,0:T(8,128)(2,1)} %get-tuple-element.884) | copy-start | bytes 6291460 | tf_op jit(solution)/shard_map/while
  1120.0 90.2 %collective-permute-start = (bf16[16,128,1024]{2,1,0:T(8,128)(2,1)}, bf16[16,128,1024]{2,1,0:T(8,128)(2,1)}, u32[]{:S(2)}, u32[]{:S(2)}) collective-permute-start(bf16[16,128,1024]{2,1,0:T(8,128)(2,1)} %get-tuple-element.824), channel_id=1, source_target_pairs={{0,2},{2,4},{4,6},{1,3},{3,5},{5,7}} | collective-permute-start | bytes 12582920 | tf_op jit(solution)/shard_map/while/body/eval_jaxpr/ppermute | solution.py:129
  1129.4 171.5 %collective-permute-start.1 = (bf16[16,128,1024]{2,1,0:T(8,128)(2,1)}, bf16[16,128,1024]{2,1,0:T(8,128)(2,1)}, u32[]{:S(2)}, u32[]{:S(2)}) collective-permute-start(bf16[16,128,1024]{2,1,0:T(8,128)(2,1)} %get-tuple-element.740), channel_id=1, source_target_pairs={{2,0},{4,2},{6,4},{3,1},{5,3},{7,5}} | collective-permute-start | bytes 12582920 | tf_op jit(solution)/shard_map/while/body/eval_jaxpr/ppermute | solution.py:130
  1134.2 166.7 %copy-start.22 = (bf16[1,1024,1024]{2,1,0:T(8,128)(2,1)S(1)}, bf16[1,1024,1024]{2,1,0:T(8,128)(2,1)}, u32[]{:S(2)}) copy-start(bf16[1,1024,1024]{2,1,0:T(8,128)(2,1)} %get-tuple-element.884) | copy-start | bytes 6291460 | tf_op jit(solution)/shard_map/while
  1433.0 89.6 %collective-permute-start = (bf16[16,128,1024]{2,1,0:T(8,128)(2,1)}, bf16[16,128,1024]{2,1,0:T(8,128)(2,1)}, u32[]{:S(2)}, u32[]{:S(2)}) collective-permute-start(bf16[16,128,1024]{2,1,0:T(8,128)(2,1)} %get-tuple-element.824), channel_id=1, source_target_pairs={{0,2},{2,4},{4,6},{1,3},{3,5},{5,7}} | collective-permute-start | bytes 12582920 | tf_op jit(solution)/shard_map/while/body/eval_jaxpr/ppermute | solution.py:129
  1442.3 293.1 %collective-permute-start.1 = (bf16[16,128,1024]{2,1,0:T(8,128)(2,1)}, bf16[16,128,1024]{2,1,0:T(8,128)(2,1)}, u32[]{:S(2)}, u32[]{:S(2)}) collective-permute-start(bf16[16,128,1024]{2,1,0:T(8,128)(2,1)} %get-tuple-element.740), channel_id=1, source_target_pairs={{2,0},{4,2},{6,4},{3,1},{5,3},{7,5}} | collective-permute-start | bytes 12582920 | tf_op jit(solution)/shard_map/while/body/eval_jaxpr/ppermute | solution.py:130
  1447.1 288.3 %copy-start.22 = (bf16[1,1024,1024]{2,1,0:T(8,128)(2,1)S(1)}, bf16[1,1024,1024]{2,1,0:T(8,128)(2,1)}, u32[]{:S(2)}) copy-start(bf16[1,1024,1024]{2,1,0:T(8,128)(2,1)} %get-tuple-element.884) | copy-start | bytes 6291460 | tf_op jit(solution)/shard_map/while
  1867.6 374.0 %collective-permute-start = (bf16[16,128,1024]{2,1,0:T(8,128)(2,1)}, bf16[16,128,1024]{2,1,0:T(8,128)(2,1)}, u32[]{:S(2)}, u32[]{:S(2)}) collective-permute-start(bf16[16,128,1024]{2,1,0:T(8,128)(2,1)} %get-tuple-element.824), channel_id=1, source_target_pairs={{0,2},{2,4},{4,6},{1,3},{3,5},{5,7}} | collective-permute-start | bytes 12582920 | tf_op jit(solution)/shard_map/while/body/eval_jaxpr/ppermute | solution.py:129
  2162.7 455.4 %collective-permute-start.1 = (bf16[16,128,1024]{2,1,0:T(8,128)(2,1)}, bf16[16,128,1024]{2,1,0:T(8,128)(2,1)}, u32[]{:S(2)}, u32[]{:S(2)}) collective-permute-start(bf16[16,128,1024]{2,1,0:T(8,128)(2,1)} %get-tuple-element.740), channel_id=1, source_target_pairs={{2,0},{4,2},{6,4},{3,1},{5,3},{7,5}} | collective-permute-start | bytes 12582920 | tf_op jit(solution)/shard_map/while/body/eval_jaxpr/ppermute | solution.py:130
  2167.4 450.7 %copy-start.22 = (bf16[1,1024,1024]{2,1,0:T(8,128)(2,1)S(1)}, bf16[1,1024,1024]{2,1,0:T(8,128)(2,1)}, u32[]{:S(2)}) copy-start(bf16[1,1024,1024]{2,1,0:T(8,128)(2,1)} %get-tuple-element.884) | copy-start | bytes 6291460 | tf_op jit(solution)/shard_map/while
  2640.4 498.6 %collective-permute-start = (bf16[16,128,1024]{2,1,0:T(8,128)(2,1)}, bf16[16,128,1024]{2,1,0:T(8,128)(2,1)}, u32[]{:S(2)}, u32[]{:S(2)}) collective-permute-start(bf16[16,128,1024]{2,1,0:T(8,128)(2,1)} %get-tuple-element.824), channel_id=1, source_target_pairs={{0,2},{2,4},{4,6},{1,3},{3,5},{5,7}} | collective-permute-start | bytes 12582920 | tf_op jit(solution)/shard_map/while/body/eval_jaxpr/ppermute | solution.py:129
  2757.5 78.3 %copy-start.23 = (bf16[1,1024,1024]{2,1,0:T(8,128)(2,1)}, bf16[1,1024,1024]{2,1,0:T(8,128)(2,1)S(1)}, u32[]{:S(2)}) copy-start(bf16[1,1024,1024]{2,1,0:T(8,128)(2,1)S(1)} %get-tuple-element.525) | copy-start | bytes 6291460 | tf_op jit(solution)/shard_map/while/body/eval_jaxpr/cond
  2871.5 43.6 copy-start.7
  2974.4 43.1 copy-start.4
  3130.0 89.0 %collective-permute-start.1 = (bf16[16,128,1024]{2,1,0:T(8,128)(2,1)}, bf16[16,128,1024]{2,1,0:T(8,128)(2,1)}, u32[]{:S(2)}, u32[]{:S(2)}) collective-permute-start(bf16[16,128,1024]{2,1,0:T(8,128)(2,1)} %get-tuple-element.740), channel_id=1, source_target_pairs={{2,0},{4,2},{6,4},{3,1},{5,3},{7,5}} | collective-permute-start | bytes 12582920 | tf_op jit(solution)/shard_map/while/body/eval_jaxpr/ppermute | solution.py:130
  3134.7 84.2 %copy-start.22 = (bf16[1,1024,1024]{2,1,0:T(8,128)(2,1)S(1)}, bf16[1,1024,1024]{2,1,0:T(8,128)(2,1)}, u32[]{:S(2)}) copy-start(bf16[1,1024,1024]{2,1,0:T(8,128)(2,1)} %get-tuple-element.884) | copy-start | bytes 6291460 | tf_op jit(solution)/shard_map/while
  3241.2 385.6 %collective-permute-start = (bf16[16,128,1024]{2,1,0:T(8,128)(2,1)}, bf16[16,128,1024]{2,1,0:T(8,128)(2,1)}, u32[]{:S(2)}, u32[]{:S(2)}) collective-permute-start(bf16[16,128,1024]{2,1,0:T(8,128)(2,1)} %get-tuple-element.824), channel_id=1, source_target_pairs={{0,2},{2,4},{4,6},{1,3},{3,5},{5,7}} | collective-permute-start | bytes 12582920 | tf_op jit(solution)/shard_map/while/body/eval_jaxpr/ppermute | solution.py:129
  3245.3 78.3 %copy-start.23 = (bf16[1,1024,1024]{2,1,0:T(8,128)(2,1)}, bf16[1,1024,1024]{2,1,0:T(8,128)(2,1)S(1)}, u32[]{:S(2)}) copy-start(bf16[1,1024,1024]{2,1,0:T(8,128)(2,1)S(1)} %get-tuple-element.525) | copy-start | bytes 6291460 | tf_op jit(solution)/shard_map/while/body/eval_jaxpr/cond
  3359.3 43.6 copy-start.7
  3462.2 43.1 copy-start.4
  3617.8 193.6 %collective-permute-start.1 = (bf16[16,128,1024]{2,1,0:T(8,128)(2,1)}, bf16[16,128,1024]{2,1,0:T(8,128)(2,1)}, u32[]{:S(2)}, u32[]{:S(2)}) collective-permute-start(bf16[16,128,1024]{2,1,0:T(8,128)(2,1)} %get-tuple-element.740), channel_id=1, source_target_pairs={{2,0},{4,2},{6,4},{3,1},{5,3},{7,5}} | collective-permute-start | bytes 12582920 | tf_op jit(solution)/shard_map/while/body/eval_jaxpr/ppermute | solution.py:130
  3622.5 188.8 %copy-start.22 = (bf16[1,1024,1024]{2,1,0:T(8,128)(2,1)S(1)}, bf16[1,1024,1024]{2,1,0:T(8,128)(2,1)}, u32[]{:S(2)}) copy-start(bf16[1,1024,1024]{2,1,0:T(8,128)(2,1)} %get-tuple-element.884) | copy-start | bytes 6291460 | tf_op jit(solution)/shard_map/while
  3833.7 388.8 %collective-permute-start = (bf16[16,128,1024]{2,1,0:T(8,128)(2,1)}, bf16[16,128,1024]{2,1,0:T(8,128)(2,1)}, u32[]{:S(2)}, u32[]{:S(2)}) collective-permute-start(bf16[16,128,1024]{2,1,0:T(8,128)(2,1)} %get-tuple-element.824), channel_id=1, source_target_pairs={{0,2},{2,4},{4,6},{1,3},{3,5},{5,7}} | collective-permute-start | bytes 12582920 | tf_op jit(solution)/shard_map/while/body/eval_jaxpr/ppermute | solution.py:129
  3841.0 78.3 %copy-start.23 = (bf16[1,1024,1024]{2,1,0:T(8,128)(2,1)}, bf16[1,1024,1024]{2,1,0:T(8,128)(2,1)S(1)}, u32[]{:S(2)}) copy-start(bf16[1,1024,1024]{2,1,0:T(8,128)(2,1)S(1)} %get-tuple-element.525) | copy-start | bytes 6291460 | tf_op jit(solution)/shard_map/while/body/eval_jaxpr/cond
  3955.0 43.6 copy-start.7
  4057.9 43.1 copy-start.4
  4213.5 86.6 %collective-permute-start.1 = (bf16[16,128,1024]{2,1,0:T(8,128)(2,1)}, bf16[16,128,1024]{2,1,0:T(8,128)(2,1)}, u32[]{:S(2)}, u32[]{:S(2)}) collective-permute-start(bf16[16,128,1024]{2,1,0:T(8,128)(2,1)} %get-tuple-element.740), channel_id=1, source_target_pairs={{2,0},{4,2},{6,4},{3,1},{5,3},{7,5}} | collective-permute-start | bytes 12582920 | tf_op jit(solution)/shard_map/while/body/eval_jaxpr/ppermute | solution.py:130
  4218.2 81.9 %copy-start.22 = (bf16[1,1024,1024]{2,1,0:T(8,128)(2,1)S(1)}, bf16[1,1024,1024]{2,1,0:T(8,128)(2,1)}, u32[]{:S(2)}) copy-start(bf16[1,1024,1024]{2,1,0:T(8,128)(2,1)} %get-tuple-element.884) | copy-start | bytes 6291460 | tf_op jit(solution)/shard_map/while
  4322.4 491.5 %collective-permute-start = (bf16[16,128,1024]{2,1,0:T(8,128)(2,1)}, bf16[16,128,1024]{2,1,0:T(8,128)(2,1)}, u32[]{:S(2)}, u32[]{:S(2)}) collective-permute-start(bf16[16,128,1024]{2,1,0:T(8,128)(2,1)} %get-tuple-element.824), channel_id=1, source_target_pairs={{0,2},{2,4},{4,6},{1,3},{3,5},{5,7}} | collective-permute-start | bytes 12582920 | tf_op jit(solution)/shard_map/while/body/eval_jaxpr/ppermute | solution.py:129
  4432.4 78.3 %copy-start.23 = (bf16[1,1024,1024]{2,1,0:T(8,128)(2,1)}, bf16[1,1024,1024]{2,1,0:T(8,128)(2,1)S(1)}, u32[]{:S(2)}) copy-start(bf16[1,1024,1024]{2,1,0:T(8,128)(2,1)S(1)} %get-tuple-element.525) | copy-start | bytes 6291460 | tf_op jit(solution)/shard_map/while/body/eval_jaxpr/cond
  4436.9 35.8 copy-start.18
  4546.4 43.6 copy-start.7
  4649.4 43.1 copy-start.4
  4804.9 86.0 %collective-permute-start.1 = (bf16[16,128,1024]{2,1,0:T(8,128)(2,1)}, bf16[16,128,1024]{2,1,0:T(8,128)(2,1)}, u32[]{:S(2)}, u32[]{:S(2)}) collective-permute-start(bf16[16,128,1024]{2,1,0:T(8,128)(2,1)} %get-tuple-element.740), channel_id=1, source_target_pairs={{2,0},{4,2},{6,4},{3,1},{5,3},{7,5}} | collective-permute-start | bytes 12582920 | tf_op jit(solution)/shard_map/while/body/eval_jaxpr/ppermute | solution.py:130
  4809.6 81.3 %copy-start.22 = (bf16[1,1024,1024]{2,1,0:T(8,128)(2,1)S(1)}, bf16[1,1024,1024]{2,1,0:T(8,128)(2,1)}, u32[]{:S(2)}) copy-start(bf16[1,1024,1024]{2,1,0:T(8,128)(2,1)} %get-tuple-element.884) | copy-start | bytes 6291460 | tf_op jit(solution)/shard_map/while
  4913.2 386.7 %collective-permute-start = (bf16[16,128,1024]{2,1,0:T(8,128)(2,1)}, bf16[16,128,1024]{2,1,0:T(8,128)(2,1)}, u32[]{:S(2)}, u32[]{:S(2)}) collective-permute-start(bf16[16,128,1024]{2,1,0:T(8,128)(2,1)} %get-tuple-element.824), channel_id=1, source_target_pairs={{0,2},{2,4},{4,6},{1,3},{3,5},{5,7}} | collective-permute-start | bytes 12582920 | tf_op jit(solution)/shard_map/while/body/eval_jaxpr/ppermute | solution.py:129
  4918.4 78.3 %copy-start.23 = (bf16[1,1024,1024]{2,1,0:T(8,128)(2,1)}, bf16[1,1024,1024]{2,1,0:T(8,128)(2,1)S(1)}, u32[]{:S(2)}) copy-start(bf16[1,1024,1024]{2,1,0:T(8,128)(2,1)S(1)} %get-tuple-element.525) | copy-start | bytes 6291460 | tf_op jit(solution)/shard_map/while/body/eval_jaxpr/cond
  5032.4 43.6 copy-start.7
  5135.3 43.1 copy-start.4
  5290.9 84.7 %collective-permute-start.1 = (bf16[16,128,1024]{2,1,0:T(8,128)(2,1)}, bf16[16,128,1024]{2,1,0:T(8,128)(2,1)}, u32[]{:S(2)}, u32[]{:S(2)}) collective-permute-start(bf16[16,128,1024]{2,1,0:T(8,128)(2,1)} %get-tuple-element.740), channel_id=1, source_target_pairs={{2,0},{4,2},{6,4},{3,1},{5,3},{7,5}} | collective-permute-start | bytes 12582920 | tf_op jit(solution)/shard_map/while/body/eval_jaxpr/ppermute | solution.py:130
  5295.6 80.0 %copy-start.22 = (bf16[1,1024,1024]{2,1,0:T(8,128)(2,1)S(1)}, bf16[1,1024,1024]{2,1,0:T(8,128)(2,1)}, u32[]{:S(2)}) copy-start(bf16[1,1024,1024]{2,1,0:T(8,128)(2,1)} %get-tuple-element.884) | copy-start | bytes 6291460 | tf_op jit(solution)/shard_map/while
  5397.9 385.5 %collective-permute-start = (bf16[16,128,1024]{2,1,0:T(8,128)(2,1)}, bf16[16,128,1024]{2,1,0:T(8,128)(2,1)}, u32[]{:S(2)}, u32[]{:S(2)}) collective-permute-start(bf16[16,128,1024]{2,1,0:T(8,128)(2,1)} %get-tuple-element.824), channel_id=1, source_target_pairs={{0,2},{2,4},{4,6},{1,3},{3,5},{5,7}} | collective-permute-start | bytes 12582920 | tf_op jit(solution)/shard_map/while/body/eval_jaxpr/ppermute | solution.py:129
  5402.0 78.3 %copy-start.23 = (bf16[1,1024,1024]{2,1,0:T(8,128)(2,1)}, bf16[1,1024,1024]{2,1,0:T(8,128)(2,1)S(1)}, u32[]{:S(2)}) copy-start(bf16[1,1024,1024]{2,1,0:T(8,128)(2,1)S(1)} %get-tuple-element.525) | copy-start | bytes 6291460 | tf_op jit(solution)/shard_map/while/body/eval_jaxpr/cond
  5515.9 43.6 copy-start.7
  5618.9 43.1 copy-start.4
  5774.4 83.7 %collective-permute-start.1 = (bf16[16,128,1024]{2,1,0:T(8,128)(2,1)}, bf16[16,128,1024]{2,1,0:T(8,128)(2,1)}, u32[]{:S(2)}, u32[]{:S(2)}) collective-permute-start(bf16[16,128,1024]{2,1,0:T(8,128)(2,1)} %get-tuple-element.740), channel_id=1, source_target_pairs={{2,0},{4,2},{6,4},{3,1},{5,3},{7,5}} | collective-permute-start | bytes 12582920 | tf_op jit(solution)/shard_map/while/body/eval_jaxpr/ppermute | solution.py:130
  5779.2 79.0 %copy-start.22 = (bf16[1,1024,1024]{2,1,0:T(8,128)(2,1)S(1)}, bf16[1,1024,1024]{2,1,0:T(8,128)(2,1)}, u32[]{:S(2)}) copy-start(bf16[1,1024,1024]{2,1,0:T(8,128)(2,1)} %get-tuple-element.884) | copy-start | bytes 6291460 | tf_op jit(solution)/shard_map/while
  5859.6 27.3 reduce-scatter.6.cloned.1.call-start
  5860.2 52.5 reduce-scatter.10.cloned.1.call-start
  5860.9 77.6 %reduce-scatter.12.cloned.1.call-start = ((), (), s32[]{:S(2)}) async-start(), calls=%async_computation.12 | async-start | bytes 25165824 | tf_op jit(solution)/shard_map/reduce_scatter | solution.py:136
  5861.7 297.5 %reduce-scatter.14.cloned.1.call-start = ((), (), s32[]{:S(2)}) async-start(), calls=%async_computation.13 | async-start | bytes 31457280 | tf_op jit(solution)/shard_map/reduce_scatter | solution.py:138
  (138 other events, 1757.1 us)
Sparse Core Ops, SparseCore 0:
  9.5 10.6 all-gather.6
  21.7 15.7 all-gather.4
  39.0 19.1 all-gather.8
  59.6 19.1 all-gather.10
  5859.7 7.3 reduce-scatter.7
  5869.9 16.9 reduce-scatter.5
  5889.7 22.9 reduce-scatter.9
  5915.5 22.9 reduce-scatter.11
  5942.1 217.0 reduce-scatter.13
where the time goes:
time: 6170 us
  matrix products  2480 us (40%)
  waiting for transfers between devices  2240 us (36%)
  other arithmetic  582 us (9%)
  starting transfers between devices  573 us (9%)
  local copies, waits for them, and re-layouts  197 us (3%)
  loops' own time  85.4 us (1%)
    ppermute x12, waiting for transfers between devices, run_tick(): bwd_buf = lax.ppermute(ct_in, 'pp', bwd_pairs)  1440 us
    ppermute x12, starting transfers between devices, run_tick(): fwd_buf = lax.ppermute(stage_out, 'pp', fwd_pairs)  557 us
    ppermute x12, waiting for transfers between devices, run_tick(): fwd_buf = lax.ppermute(stage_out, 'pp', fwd_pairs)  432 us
    dot_general x12, matrix products, layer_forward(): jnp.einsum('bsd,df->bsf', normed2, w_up, preferred_element_type=jnp.float32)  331 us
    dot_general x24, matrix products, attn_core(): jnp.einsum('bqnh,bknh->bnqk', q_heads, k_heads, preferred_element_type=jn...  307 us
    dot_general x6, matrix products, layer_backward(): jnp.einsum('bsd,fd->bsf', ct_out, w_down, preferred_element_type=jnp.floa...  261 us
    dot_general x24, matrix products, attn_core(): jnp.einsum('bnqk,bknh->bqnh', prob_bf, v_heads, preferred_element_type=jn...  247 us
    sub x12, other arithmetic, attn_core(): jax.nn.softmax(jnp.where(causal, scores, -1e+30), axis=-1)  225 us
  transfers between devices with their start and end apart: 33, of which 26 were waited for; matrix products, arithmetic and copies ran while one was open for 38% of the time, Pallas kernels for 0%

commit v1 on v0

v1 whole, which is shorter than its diff:
```python
import functools

import jax
import jax.numpy as jnp
from jax import lax
from jax.experimental import pallas as pl
from jax.experimental.pallas import tpu as pltpu
from jax.sharding import PartitionSpec as P

EPS = 1e-6
SEQ = 128
D = 1024
CHUNK = 256
HEAD = 64
NSEQ = CHUNK // SEQ
GROUP = 256
GELU_C = 0.7978845608028654
BF = jnp.bfloat16
F32 = jnp.float32
VMEM_LIMIT = 62 * 2 ** 20
WARM = (11, 8, 4, 1)


def dot_nn(a, b):
    return lax.dot_general(a, b, (((1,), (0,)), ((), ())), preferred_element_type=F32)


def dot_nt(a, b):
    return lax.dot_general(a, b, (((1,), (1,)), ((), ())), preferred_element_type=F32)


def dot_tn(a, b):
    return lax.dot_general(a, b, (((0,), (0,)), ((), ())), preferred_element_type=F32)


def rms(v):
    return v * lax.rsqrt(jnp.mean(v * v, axis=-1, keepdims=True) + EPS)


def rms_pull(v, g):
    scale = lax.rsqrt(jnp.mean(v * v, axis=-1, keepdims=True) + EPS)
    inner = jnp.mean(v * g, axis=-1, keepdims=True)
    return scale * g - v * (scale * scale * scale * inner)


def head_masks():
    lane = lax.broadcasted_iota(jnp.int32, (1, GROUP), 1) // HEAD
    return [jnp.where(lane == h, 1.0, 0.0) for h in range(GROUP // HEAD)]


def stack_heads(x, masks):
    return jnp.concatenate([x * m.astype(BF) for m in masks], axis=0)


def probs_of(q, k_stack, causal):
    scores = dot_nt(q, k_stack) * (HEAD ** -0.5)
    out = []
    for h in range(GROUP // HEAD):
        s = jnp.where(causal, scores[:, h * SEQ:(h + 1) * SEQ], -1e30)
        e = jnp.exp(s - jnp.max(s, axis=-1, keepdims=True))
        out.append(e * (1.0 / jnp.sum(e, axis=-1, keepdims=True)))
    return out


def causal_mask():
    return lax.broadcasted_iota(jnp.int32, (SEQ, SEQ), 0) >= lax.broadcasted_iota(jnp.int32, (SEQ, SEQ), 1)


def attn_fwd(qkv, attn):
    def one_seq(n, carry):
        sl = pl.ds(pl.multiple_of(n * SEQ, SEQ), SEQ)
        masks = head_masks()
        causal = causal_mask()
        for g in range(D // GROUP):
            q, k, v = [qkv[sl, pl.ds(part * D + g * GROUP, GROUP)] for part in range(3)]
            probs = probs_of(q, stack_heads(k, masks), causal)
            prob = jnp.concatenate([p.astype(BF) for p in probs], axis=1)
            attn[sl, pl.ds(g * GROUP, GROUP)] = dot_nn(prob, stack_heads(v, masks)).astype(BF)
        return carry
    lax.fori_loop(0, NSEQ, one_seq, 0)


def attn_bwd(qkv, ct_attn, ct_qkv):
    def one_seq(n, carry):
        sl = pl.ds(pl.multiple_of(n * SEQ, SEQ), SEQ)
        masks = head_masks()
        causal = causal_mask()
        for g in range(D // GROUP):
            lanes = [pl.ds(part * D + g * GROUP, GROUP) for part in range(3)]
            q, k, v = [qkv[sl, ln] for ln in lanes]
            cta = ct_attn[sl, lanes[0]]
            k_stack = stack_heads(k, masks)
            probs = probs_of(q, k_stack, causal)
            ct_prob = dot_nt(cta, stack_heads(v, masks)).astype(BF).astype(F32)
            ds = []
            for h, p in enumerate(probs):
                pd = p * ct_prob[:, h * SEQ:(h + 1) * SEQ]
                ds.append(((pd - p * jnp.sum(pd, axis=-1, keepdims=True)) * (HEAD ** -0.5)).astype(BF))
            ds = jnp.concatenate(ds, axis=1)
            prob = jnp.concatenate([p.astype(BF) for p in probs], axis=1)
            ct_qkv[sl, lanes[0]] = dot_nn(ds, k_stack).astype(BF)
            ck = dot_tn(ds, q)
            cv = dot_tn(prob, cta)
            ct_qkv[sl, lanes[1]] = sum(ck[h * SEQ:(h + 1) * SEQ] * masks[h] for h in range(GROUP // HEAD)).astype(BF)
            ct_qkv[sl, lanes[2]] = sum(cv[h * SEQ:(h + 1) * SEQ] * masks[h] for h in range(GROUP // HEAD)).astype(BF)
        return carry
    lax.fori_loop(0, NSEQ, one_seq, 0)


def pipeline_kernel(chunks, stages, *refs):
    acts, seeds, *w_parts = refs[:6]
    (h_st, normed_st, qkv_st, attn_st, mid_st, normed2_st, up_st, gelu_st,
     ctout_st, ctup_st, ctmid_st, ctqkv_st, act_out) = refs[6:19]
    (wqkv, wproj, wup, wdown, x, normed, qkv, attn, mid, normed2, up, gelu, acc, hout,
     ct, b_h, b_qkv, b_mid, b_up, ctup, ctmid, ctattn, ctqkv, ctin,
     w_local, w_send, w_recv, f_in, f_out, b_in, b_load, b_out,
     f_send, f_recv, g_send, g_recv, o_send, o_recv, o_local) = refs[19:]
    stage = lax.axis_index('pp')
    replica = lax.axis_index('dp')
    first, last = stage == 0, stage == stages - 1
    weights = (wqkv, wproj, wup, wdown)

    def weight_copies(n):
        rows = w_parts[n].shape[0]
        mine = weights[n].at[pl.ds(pl.multiple_of(replica * rows, rows), rows)]
        return (pltpu.make_async_copy(w_parts[n], mine, w_local.at[n]),
                pltpu.make_async_remote_copy(src_ref=w_parts[n], dst_ref=mine, send_sem=w_send.at[n], recv_sem=w_recv.at[n],
                                             device_id=(stage, 1 - replica), device_id_type=pl.DeviceIdType.MESH))

    for n in range(4):
        for copy in weight_copies(n):
            copy.start()

    def wait_weight(n, i):
        @pl.when(i == 0)
        def _():
            for copy in weight_copies(n):
                copy.wait()

    def send_h(i):
        return pltpu.make_async_remote_copy(
            src_ref=hout, dst_ref=h_st.at[i], send_sem=f_send, recv_sem=f_recv.at[i],
            device_id=(jnp.minimum(stage + 1, stages - 1), replica), device_id_type=pl.DeviceIdType.MESH)

    def send_ct(i):
        return pltpu.make_async_remote_copy(
            src_ref=ctin, dst_ref=ctout_st.at[i], send_sem=g_send, recv_sem=g_recv.at[i],
            device_id=(jnp.maximum(stage - 1, 0), replica), device_id_type=pl.DeviceIdType.MESH)

    part = SEQ // stages

    def send_out(i, s):
        return pltpu.make_async_remote_copy(
            src_ref=hout.at[:, pl.ds(s * part, part)], dst_ref=act_out.at[pl.ds(i * NSEQ, NSEQ)],
            send_sem=o_send.at[s], recv_sem=o_recv, device_id=(s, replica), device_id_type=pl.DeviceIdType.MESH)

    def keep_out(i):
        return pltpu.make_async_copy(hout.at[:, pl.ds((stages - 1) * part, part)], act_out.at[pl.ds(i * NSEQ, NSEQ)], o_local)

    f_bufs = ((normed, normed_st), (qkv, qkv_st), (attn, attn_st), (mid, mid_st), (normed2, normed2_st), (up, up_st), (gelu, gelu_st))
    b_bufs = ((ctup, ctup_st), (ctmid, ctmid_st), (ctqkv, ctqkv_st))

    def f_save(n, i):
        return pltpu.make_async_copy(f_bufs[n][0], f_bufs[n][1].at[i], f_out.at[n])

    def b_save(n, i):
        return pltpu.make_async_copy(b_bufs[n][0], b_bufs[n][1].at[i], b_out.at[n])

    def seed_save(i):
        return pltpu.make_async_copy(ct, ctout_st.at[i], b_out.at[3])

    def b_loads(i):
        return [pltpu.make_async_copy(qkv_st.at[i], b_qkv, b_load.at[0]),
                pltpu.make_async_copy(mid_st.at[i], b_mid, b_load.at[1]),
                pltpu.make_async_copy(up_st.at[i], b_up, b_load.at[2])]

    def either(cond, src_yes, src_no, dst, sem):
        @pl.when(cond)
        def _():
            pltpu.make_async_copy(src_yes, dst, sem).start()

        @pl.when(jnp.logical_not(cond))
        def _():
            pltpu.make_async_copy(src_no, dst, sem).start()

    def wait_sent_h(i):
        @pl.when(jnp.logical_not(last))
        def _():
            send_h(i).wait_send()

        @pl.when(last)
        def _():
            for s in range(stages - 1):
                send_out(i, s).wait_send()
            keep_out(i).wait()

    def wait_b_saves(i):
        for n in range(3):
            b_save(n, i).wait()

        @pl.when(last)
        def _():
            seed_save(i).wait()

    def forward(i):
        @pl.when(jnp.logical_not(first))
        def _():
            send_h(i).wait_recv()
        either(first, acts.at[i], h_st.at[i], x, f_in)
        wait_weight(0, i)
        pltpu.make_async_copy(acts.at[i], x, f_in).wait()
        hid = x[...].reshape(CHUNK, D).astype(F32)
        normed[...] = rms(hid).astype(BF)
        f_save(0, i).start()
        for n in range(3):
            ln = pl.ds(n * D, D)
            qkv[:, ln] = dot_nn(normed[...], wqkv[:, ln]).astype(BF)
        f_save(1, i).start()
        attn_fwd(qkv, attn)
        f_save(2, i).start()
        wait_weight(1, i)
        mid[...] = (x[...].reshape(CHUNK, D).astype(F32) + dot_nn(attn[...], wproj[...])).astype(BF)
        f_save(3, i).start()
        normed2[...] = rms(mid[...].astype(F32)).astype(BF)
        f_save(4, i).start()
        wait_weight(2, i)
        for n in range(4):
            ln = pl.ds(n * D, D)
            up_act = dot_nn(normed2[...], wup[:, ln]).astype(BF)
            up[:, ln] = up_act
            v = up_act.astype(F32)
            t = jnp.tanh(v * (GELU_C + (GELU_C * 0.044715) * (v * v)))
            gelu[:, ln] = (v * (0.5 + 0.5 * t)).astype(BF)
        f_save(5, i).start()
        f_save(6, i).start()
        wait_weight(3, i)
        acc[...] = mid[...].astype(F32) + dot_nn(gelu[...], wdown[...])

        @pl.when(i > 0)
        def _():
            wait_sent_h(i - 1)
        hout[...] = acc[...].astype(BF).reshape(NSEQ, SEQ, D)

        @pl.when(jnp.logical_not(last))
        def _():
            send_h(i).start()

        @pl.when(last)
        def _():
            for s in range(stages - 1):
                send_out(i, s).start()
            keep_out(i).start()

    def backward(i):
        @pl.when(i > 0)
        def _():
            wait_b_saves(i - 1)

        @pl.when(jnp.logical_not(last))
        def _():
            send_ct(i).wait_recv()
        either(last, seeds.at[i], ctout_st.at[i], ct, b_in)
        for copy in b_loads(i):
            copy.wait()
        pltpu.make_async_copy(seeds.at[i], ct, b_in).wait()

        @pl.when(last)
        def _():
            seed_save(i).start()
        for n in range(4):
            ln = pl.ds(n * D, D)
            ct_gelu = dot_nt(ct[...].reshape(CHUNK, D), wdown[ln, :]).astype(BF).astype(F32)
            v = b_up[:, ln].astype(F32)
            v2 = v * v
            t = jnp.tanh(v * (GELU_C + (GELU_C * 0.044715) * v2))
            slope = 0.5 * (1.0 + t) + (0.5 * v) * (1.0 - t * t) * (GELU_C + (GELU_C * 3 * 0.044715) * v2)
            ctup[:, ln] = (ct_gelu * slope).astype(BF)
        b_save(0, i).start()
        acc[...] = dot_nt(ctup[...], wup[...])
        ct_norm2 = acc[...].astype(BF).astype(F32)
        ctmid[...] = (ct[...].reshape(CHUNK, D).astype(F32) + rms_pull(b_mid[...].astype(F32), ct_norm2)).astype(BF)
        b_save(1, i).start()
        ctattn[...] = dot_nt(ctmid[...], wproj[...]).astype(BF)
        attn_bwd(b_qkv, ctattn, ctqkv)
        b_save(2, i).start()
        pltpu.make_async_copy(acts.at[i], b_h, b_load.at[3]).wait()

        @pl.when(jnp.logical_not(first))
        def _():
            acc[...] = dot_nt(ctqkv[...], wqkv[...])

            @pl.when(i > 0)
            def _():
                send_ct(i - 1).wait_send()
            ct_norm = acc[...].astype(BF).astype(F32)
            ct_hid = ctmid[...].astype(F32) + rms_pull(b_h[...].reshape(CHUNK, D).astype(F32), ct_norm)
            ctin[...] = ct_hid.astype(BF).reshape(NSEQ, SEQ, D)
            send_ct(i).start()

    warm = jnp.int32(WARM[stages - 1])
    for s in range(stages - 1):
        warm = jnp.where(stage == s, WARM[s], warm)

    def tick(t, carry):
        @pl.when((t >= 1) & (t <= chunks))
        def _():
            for n in range(7):
                f_save(n, t - 1).wait()
        j = t - warm
        b_ok = (j >= 0) & (j < chunks)

        @pl.when(b_ok)
        def _():
            for copy in b_loads(j):
                copy.start()
            either(first, acts.at[j], h_st.at[j], b_h, b_load.at[3])

        @pl.when(t < chunks)
        def _():
            forward(t)

        @pl.when(b_ok)
        def _():
            backward(j)
        return carry

    lax.fori_loop(0, chunks + max(WARM), tick, 0)
    wait_sent_h(chunks - 1)
    wait_b_saves(chunks - 1)

    @pl.when(jnp.logical_not(first))
    def _():
        send_ct(chunks - 1).wait_send()

    @pl.when(jnp.logical_not(last))
    def _():
        pltpu.make_async_copy(act_out, act_out, o_recv).wait()


ANY = pl.BlockSpec(memory_space=pl.ANY)


def run_pipeline(acts, seeds, w_parts, stages):
    chunks = acts.shape[0]

    def stash(width):
        return jax.ShapeDtypeStruct((chunks, CHUNK, width), BF)

    def vmem(*shape):
        return pltpu.VMEM(shape, BF)

    whole = (NSEQ, SEQ, D)
    like_acts = jax.ShapeDtypeStruct(acts.shape, BF)
    out_shape = [like_acts, stash(D), stash(3 * D), stash(D), stash(D), stash(D), stash(4 * D), stash(4 * D),
                 like_acts, stash(4 * D), stash(D), stash(3 * D),
                 jax.ShapeDtypeStruct((chunks * NSEQ, SEQ // stages, D), BF)]
    dma = pltpu.SemaphoreType.DMA
    scratch = [
        vmem(D, 3 * D), vmem(D, D), vmem(D, 4 * D), vmem(4 * D, D),
        vmem(*whole), vmem(CHUNK, D), vmem(CHUNK, 3 * D), vmem(CHUNK, D), vmem(CHUNK, D), vmem(CHUNK, D),
        vmem(CHUNK, 4 * D), vmem(CHUNK, 4 * D), pltpu.VMEM((CHUNK, D), F32), vmem(*whole),
        vmem(*whole), vmem(*whole), vmem(CHUNK, 3 * D), vmem(CHUNK, D), vmem(CHUNK, 4 * D), vmem(CHUNK, 4 * D),
        vmem(CHUNK, D), vmem(CHUNK, D), vmem(CHUNK, 3 * D), vmem(*whole),
        dma((4,)), dma((4,)), dma((4,)), dma, dma((7,)), dma, dma((4,)), dma((4,)),
        dma, dma((chunks,)), dma, dma((chunks,)), dma((stages - 1,)), dma, dma,
    ]
    return pl.pallas_call(
        functools.partial(pipeline_kernel, chunks, stages),
        in_specs=[ANY] * 6, out_specs=[ANY] * len(out_shape), out_shape=out_shape, scratch_shapes=scratch,
        compiler_params=pltpu.CompilerParams(has_side_effects=True, vmem_limit_bytes=VMEM_LIMIT),
        cost_estimate=pl.CostEstimate(flops=chunks * CHUNK * 24 * D * D * 2, bytes_accessed=10 ** 9, transcendentals=chunks * CHUNK * 12 * D),
        name='pipeline',
    )(acts, seeds, *w_parts)


def solution(mesh):
    stages = mesh.shape['pp']

    def device_step(act_in, loss_seed, w_qkv, w_proj, w_up, w_down):
        tokens = act_in.shape[0] * act_in.shape[1] * act_in.shape[2]
        acts = act_in.reshape(-1, NSEQ, SEQ, D)
        seeds = loss_seed.reshape(-1, NSEQ, SEQ, D)
        w_parts = (w_qkv[0].reshape(-1, 3 * D), w_proj[0], w_up[0], w_down[0])
        outs = run_pipeline(acts, seeds, w_parts, stages)
        act_out = outs[12].reshape(act_in.shape[0], act_in.shape[1], -1, D)
        (_, normed, _, attn, _, normed2, _, gelu, ct_out, ct_up, ct_mid, ct_qkv) = [
            a.reshape(tokens, -1) for a in outs[:12]]

        def weight_grad(lhs, rhs):
            return lax.psum_scatter(dot_tn(lhs, rhs), 'dp', scatter_dimension=0, tiled=True)

        g_down = weight_grad(gelu, ct_out)
        g_up = weight_grad(normed2, ct_up)
        g_qkv = weight_grad(normed, ct_qkv)
        g_proj = weight_grad(attn, ct_mid)
        return g_qkv.reshape(w_qkv.shape), g_proj[None], g_up[None], g_down[None], act_out

    weight_spec = P('pp', 'dp')
    act_spec = P(None, 'dp')
    return jax.shard_map(device_step, mesh=mesh, in_specs=(act_spec, act_spec, weight_spec, weight_spec, weight_spec, weight_spec), out_specs=(weight_spec, weight_spec, weight_spec, weight_spec, P(None, 'dp', 'pp')), check_vma=False)
```

time: 6170 us -> 2050 us (0.33)
  waiting for transfers between devices: 2240 us -> 14.1 us
  matrix products: 2480 us -> 356 us
  Pallas kernels: 0 us -> 1640 us
  other arithmetic: 582 us -> 0 us
  starting transfers between devices: 573 us -> 0.16 us
  local copies, waits for them, and re-layouts: 197 us -> 18 us
  loops' own time: 85.4 us -> 0 us
    dot_general x138 -> x4, matrix products: 2480 us -> 356 us  [dot_tn(): lax.dot_general(a, b, (((0,), (0,)), ((), ())), preferred_element_type=F32)]
    ppermute x24 -> x0, waiting for transfers between devices: 1870 us -> none  [the longest x12 1440 us: run_tick(): bwd_buf = lax.ppermute(ct_in, 'pp', bwd_pairs)]
    pallas_call x0 -> x1, Pallas kernels: none -> 1640 us  [run_pipeline(): pl.pallas_call(functools.partial(pipeline_kernel, chunks, stages), in_spe...]
    ppermute x24 -> x0, starting transfers between devices: 572 us -> none  [the longest x12 557 us: run_tick(): fwd_buf = lax.ppermute(stage_out, 'pp', fwd_pairs)]
    reduce_scatter x5 -> x4, waiting for transfers between devices: 288 us -> 14 us  [weight_grad(): lax.psum_scatter(dot_tn(lhs, rhs), 'dp', scatter_dimension=0, tiled=True)]
    sub x12 -> x0, other arithmetic: 225 us -> none  [attn_core(): jax.nn.softmax(jnp.where(causal, scores, -1e+30), axis=-1)]
    dynamic_update_slice x24 -> x0, other arithmetic: 135 us -> none  [the longest x12 83.7 us: run_tick(): lax.dynamic_update_index_in_dim(stash_in, jnp.where(fwd_ok, stage_in, old...]
    convert_element_type x18 -> x0, other arithmetic: 130 us -> none  [the longest x6 57.7 us: attn_core(): jax.nn.softmax(jnp.where(causal, scores, -1e+30), axis=-1)]
  transfers between devices with their start and end apart: 33 -> 4, of which waited for: 26 -> 1; matrix products, arithmetic and copies ran while one was open for 38% -> 13% of each run, Pallas kernels for 0% -> 0%
where the time goes in v1:
time: 2050 us; the launch traced here: 2040 us
  Pallas kernels  1640 us (80%)
  matrix products  356 us (17%)
    pallas_call x1, Pallas kernels, run_pipeline(): pl.pallas_call(functools.partial(pipeline_kernel, chunks, stages), in_spe...  1640 us
    dot_general x4, matrix products, dot_tn(): lax.dot_general(a, b, (((0,), (0,)), ((), ())), preferred_element_type=F32)  356 us
  transfers between devices with their start and end apart: 4, of which 1 were waited for; matrix products, arithmetic and copies ran while one was open for 13% of the time, Pallas kernels for 0%

profile of v1, /device:TPU:0, one launch (start us, length us, event | category | flops | bytes accessed | tf_op | source)
XLA Modules:
  0.0 2038.0 jit_solution(9027294568708833140)
XLA Ops:
  7.2 0.0 reduce-scatter.5.cloned.1.call-start
  7.2 4.6 copy.16.refs_2_
  11.8 1636.0 %pipeline.1 = (bf16[48,2,128,1024]{3,2,1,0:T(8,128)(2,1)}, bf16[48,256,1024]{2,1,0:T(8,128)(2,1)}, bf16[48,256,3072]{2,1,0:T(8,128)(2,1)}, bf16[48,256,1024]{2,1...) custom-call(bf16[48,2,128,1024]{3,2,1,0:T(8,128)(2,1)} %bitcast.30, ...), custom_call_target="tpu_custom_call" | custom-call | flops 618475290624 | bytes 1000000000 | tf_op jit(solution)/shard_map/pipeline/pallas_call | solution.py:367
  1647.8 88.9 %convolution_bitcast_fusion.1 = f32[1024,3072]{1,0:T(8,128)} fusion(bf16[48,256,1024]{2,1,0:T(8,128)(2,1)} %get-tuple-element.14, bf16[48,256,3072]{2,1,0:T(8,128)(2,1)} %get-tuple-element.15), kind=kOutput, calls=%fused_computation.1 | convolution fusion | flops 77309411328 | bytes 113246208 | tf_op jit(solution)/shard_map/dot_general | solution.py:33
  1736.7 0.0 reduce-scatter.5.cloned.1.call-update
  1736.7 0.0 reduce-scatter.7.cloned.1.call-start
  1736.8 33.0 %convolution_bitcast_fusion.2 = f32[1024,1024]{1,0:T(8,128)} fusion(bf16[48,256,1024]{2,1,0:T(8,128)(2,1)} %get-tuple-element.16, bf16[48,256,1024]{2,1,0:T(8,128)(2,1)} %get-tuple-element.17), kind=kOutput, calls=%fused_computation.2 | convolution fusion | flops 25769803776 | bytes 54525952 | tf_op jit(solution)/shard_map/dot_general | solution.py:33
  1769.8 0.0 reduce-scatter.7.cloned.1.call-update
  1769.8 0.0 reduce-scatter.9.cloned.1.call-start
  1769.9 117.1 %convolution_bitcast_fusion = f32[1024,4096]{1,0:T(8,128)} fusion(bf16[48,256,1024]{2,1,0:T(8,128)(2,1)} %get-tuple-element.18, bf16[48,256,4096]{2,1,0:T(8,128)(2,1)} %get-tuple-element.19), kind=kOutput, calls=%fused_computation | convolution fusion | flops 103079215104 | bytes 142606336 | tf_op jit(solution)/shard_map/dot_general | solution.py:33
  1887.0 0.0 reduce-scatter.9.cloned.1.call-update
  1887.0 0.0 reduce-scatter.11.cloned.1.call-start
  1887.1 116.6 %fusion = f32[4096,1024]{1,0:T(8,128)} fusion(bf16[12288,4096]{1,0:T(8,128)(2,1)} %bitcast.12, bf16[12288,1024]{1,0:T(8,128)(2,1)} %bitcast.38), kind=kOutput, calls=%fused_computation.3 | convolution fusion | flops 103079215104 | bytes 142606336 | tf_op jit(solution)/shard_map/dot_general | solution.py:33
  2003.7 0.0 reduce-scatter.11.cloned.1.call-update
  2003.7 0.0 reduce-scatter.5.cloned.1.call-done
  2003.7 6.6 copy.18
  2010.3 0.0 reduce-scatter.7.cloned.1.call-done
  2010.3 0.0 reduce-scatter.9.cloned.1.call-done
  2010.3 14.0 reduce-scatter.11.cloned.1.call-done
  2024.3 6.8 copy.25
Async XLA Ops:
  7.2 1996.6 %reduce-scatter.5.cloned.1.call-start = ((), (), s32[]{:S(2)}) async-start(), calls=%async_computation.4 | async-start | bytes 18874368 | tf_op jit(solution)/shard_map/reduce_scatter | solution.py:390
  1736.7 273.6 %reduce-scatter.7.cloned.1.call-start = ((), (), s32[]{:S(2)}) async-start(), calls=%async_computation.5 | async-start | bytes 6291456 | tf_op jit(solution)/shard_map/reduce_scatter | solution.py:390
  1769.8 240.5 %reduce-scatter.9.cloned.1.call-start = ((), (), s32[]{:S(2)}) async-start(), calls=%async_computation.6 | async-start | bytes 25165824 | tf_op jit(solution)/shard_map/reduce_scatter | solution.py:390
  1887.0 137.3 %reduce-scatter.11.cloned.1.call-start = ((), (), s32[]{:S(2)}) async-start(), calls=%async_computation.7 | async-start | bytes 25165824 | tf_op jit(solution)/shard_map/reduce_scatter | solution.py:390
Sparse Core Ops, SparseCore 0:
  1736.8 14.4 reduce-scatter.4
  1769.9 7.3 reduce-scatter.6
  1887.1 20.4 reduce-scatter.8
  2003.8 20.4 reduce-scatter.10

commit v2 on v1

--- a/solution.py
+++ b/solution.py
@@ -13,7 +13,9 @@
 CHUNK = 256
 HEAD = 64
 NSEQ = CHUNK // SEQ
-GROUP = 256
+SCALE = HEAD ** -0.5
+FWD_LANES = 128
+BWD_LANES = 256
 GELU_C = 0.7978845608028654
 BF = jnp.bfloat16
 F32 = jnp.float32
@@ -43,39 +45,36 @@
     return scale * g - v * (scale * scale * scale * inner)
 
 
-def head_masks():
-    lane = lax.broadcasted_iota(jnp.int32, (1, GROUP), 1) // HEAD
-    return [jnp.where(lane == h, 1.0, 0.0) for h in range(GROUP // HEAD)]
-
-
-def stack_heads(x, masks):
-    return jnp.concatenate([x * m.astype(BF) for m in masks], axis=0)
-
-
-def probs_of(q, k_stack, causal):
-    scores = dot_nt(q, k_stack) * (HEAD ** -0.5)
-    out = []
-    for h in range(GROUP // HEAD):
-        s = jnp.where(causal, scores[:, h * SEQ:(h + 1) * SEQ], -1e30)
-        e = jnp.exp(s - jnp.max(s, axis=-1, keepdims=True))
-        out.append(e * (1.0 / jnp.sum(e, axis=-1, keepdims=True)))
-    return out
-
-
-def causal_mask():
-    return lax.broadcasted_iota(jnp.int32, (SEQ, SEQ), 0) >= lax.broadcasted_iota(jnp.int32, (SEQ, SEQ), 1)
+def stack_heads(x, gain):
+    lane = lax.broadcasted_iota(jnp.int32, (1, x.shape[1]), 1) // HEAD
+    return jnp.concatenate([x * jnp.where(lane == h, gain, 0.0).astype(BF) for h in range(x.shape[1] // HEAD)], axis=0)
+
+
+def pick_heads(stacked):
+    low = lax.broadcasted_iota(jnp.int32, (SEQ, 2 * HEAD), 1) < HEAD
+    cols = []
+    for p in range(stacked.shape[1] // (2 * HEAD)):
+        lanes = slice(p * 2 * HEAD, (p + 1) * 2 * HEAD)
+        row = 2 * p * SEQ
+        cols.append(jnp.where(low, stacked[row:row + SEQ, lanes], stacked[row + SEQ:row + 2 * SEQ, lanes]))
+    return cols[0] if len(cols) == 1 else jnp.concatenate(cols, axis=1)
+
+
+def probs_of(k, q_stack):
+    shape = (SEQ, q_stack.shape[0])
+    seen = lax.broadcasted_iota(jnp.int32, shape, 0) <= lax.broadcasted_iota(jnp.int32, shape, 1) % SEQ
+    s = jnp.where(seen, dot_nt(k, q_stack), -1e30)
+    e = jnp.exp(s - jnp.max(s, axis=0, keepdims=True))
+    return e * (1.0 / jnp.sum(e, axis=0, keepdims=True))
 
 
 def attn_fwd(qkv, attn):
     def one_seq(n, carry):
         sl = pl.ds(pl.multiple_of(n * SEQ, SEQ), SEQ)
-        masks = head_masks()
-        causal = causal_mask()
-        for g in range(D // GROUP):
-            q, k, v = [qkv[sl, pl.ds(part * D + g * GROUP, GROUP)] for part in range(3)]
-            probs = probs_of(q, stack_heads(k, masks), causal)
-            prob = jnp.concatenate([p.astype(BF) for p in probs], axis=1)
-            attn[sl, pl.ds(g * GROUP, GROUP)] = dot_nn(prob, stack_heads(v, masks)).astype(BF)
+        for g in range(D // FWD_LANES):
+            q, k, v = [qkv[sl, pl.ds(part * D + g * FWD_LANES, FWD_LANES)] for part in range(3)]
+            prob = probs_of(k, stack_heads(q, SCALE)).astype(BF)
+            attn[sl, pl.ds(g * FWD_LANES, FWD_LANES)] = pick_heads(dot_tn(prob, v)).astype(BF)
         return carry
     lax.fori_loop(0, NSEQ, one_seq, 0)
 
@@ -83,26 +82,18 @@
 def attn_bwd(qkv, ct_attn, ct_qkv):
     def one_seq(n, carry):
         sl = pl.ds(pl.multiple_of(n * SEQ, SEQ), SEQ)
-        masks = head_masks()
-        causal = causal_mask()
-        for g in range(D // GROUP):
-            lanes = [pl.ds(part * D + g * GROUP, GROUP) for part in range(3)]
+        for g in range(D // BWD_LANES):
+            lanes = [pl.ds(part * D + g * BWD_LANES, BWD_LANES) for part in range(3)]
             q, k, v = [qkv[sl, ln] for ln in lanes]
-            cta = ct_attn[sl, lanes[0]]
-            k_stack = stack_heads(k, masks)
-            probs = probs_of(q, k_stack, causal)
-            ct_prob = dot_nt(cta, stack_heads(v, masks)).astype(BF).astype(F32)
-            ds = []
-            for h, p in enumerate(probs):
-                pd = p * ct_prob[:, h * SEQ:(h + 1) * SEQ]
-                ds.append(((pd - p * jnp.sum(pd, axis=-1, keepdims=True)) * (HEAD ** -0.5)).astype(BF))
-            ds = jnp.concatenate(ds, axis=1)
-            prob = jnp.concatenate([p.astype(BF) for p in probs], axis=1)
-            ct_qkv[sl, lanes[0]] = dot_nn(ds, k_stack).astype(BF)
-            ck = dot_tn(ds, q)
-            cv = dot_tn(prob, cta)
-            ct_qkv[sl, lanes[1]] = sum(ck[h * SEQ:(h + 1) * SEQ] * masks[h] for h in range(GROUP // HEAD)).astype(BF)
-            ct_qkv[sl, lanes[2]] = sum(cv[h * SEQ:(h + 1) * SEQ] * masks[h] for h in range(GROUP // HEAD)).astype(BF)
+            q_stack = stack_heads(q, SCALE)
+            ct_stack = stack_heads(ct_attn[sl, lanes[0]], 1.0)
+            p = probs_of(k, q_stack)
+            ct_prob = dot_nt(v, ct_stack).astype(BF).astype(F32)
+            pd = p * ct_prob
+            ds = (pd - p * jnp.sum(pd, axis=0, keepdims=True)).astype(BF)
+            ct_qkv[sl, lanes[2]] = dot_nn(p.astype(BF), ct_stack).astype(BF)
+            ct_qkv[sl, lanes[1]] = dot_nn(ds, q_stack).astype(BF)
+            ct_qkv[sl, lanes[0]] = (pick_heads(dot_tn(ds, k)) * SCALE).astype(BF)
         return carry
     lax.fori_loop(0, NSEQ, one_seq, 0)
 
@@ -198,15 +189,23 @@
         for n in range(3):
             b_save(n, i).wait()
 
-        @pl.when(last)
-        def _():
-            seed_save(i).wait()
-
-    def forward(i):
+    def fetch_x(i):
         @pl.when(jnp.logical_not(first))
         def _():
             send_h(i).wait_recv()
         either(first, acts.at[i], h_st.at[i], x, f_in)
+
+    def fetch_ct(i):
+        @pl.when(jnp.logical_not(last))
+        def _():
+            send_ct(i).wait_recv()
+
+        @pl.when(last & (i > 0))
+        def _():
+            seed_save(i - 1).wait()
+        either(last, seeds.at[i], ctout_st.at[i], ct, b_in)
+
+    def forward(i, j, b_ok):
         wait_weight(0, i)
         pltpu.make_async_copy(acts.at[i], x, f_in).wait()
         hid = x[...].reshape(CHUNK, D).astype(F32)
@@ -234,6 +233,10 @@
         f_save(5, i).start()
         f_save(6, i).start()
         wait_weight(3, i)
+
+        @pl.when(b_ok)
+        def _():
+            fetch_ct(j)
         acc[...] = mid[...].astype(F32) + dot_nn(gelu[...], wdown[...])
 
         @pl.when(i > 0)
@@ -251,15 +254,15 @@
                 send_out(i, s).start()
             keep_out(i).start()
 
+        @pl.when(i + 1 < chunks)
+        def _():
+            fetch_x(i + 1)
+
     def backward(i):
         @pl.when(i > 0)
         def _():
             wait_b_saves(i - 1)
 
-        @pl.when(jnp.logical_not(last))
-        def _():
-            send_ct(i).wait_recv()
-        either(last, seeds.at[i], ctout_st.at[i], ct, b_in)
         for copy in b_loads(i):
             copy.wait()
         pltpu.make_async_copy(seeds.at[i], ct, b_in).wait()
@@ -317,16 +320,25 @@
 
         @pl.when(t < chunks)
         def _():
-            forward(t)
+            forward(t, j, b_ok)
+
+        @pl.when(b_ok & (t >= chunks))
+        def _():
+            fetch_ct(j)
 
         @pl.when(b_ok)
         def _():
             backward(j)
         return carry
 
+    fetch_x(0)
     lax.fori_loop(0, chunks + max(WARM), tick, 0)
     wait_sent_h(chunks - 1)
     wait_b_saves(chunks - 1)
+
+    @pl.when(last)
+    def _():
+        seed_save(chunks - 1).wait()
 
     @pl.when(jnp.logical_not(first))
     def _():

time: 2050 us -> 1710 us (0.83)
  Pallas kernels: 1640 us -> 1290 us
    pallas_call x1, Pallas kernels: 1640 us -> 1290 us  [run_pipeline(): pl.pallas_call(functools.partial(pipeline_kernel, chunks, stages), in_spe...]
  transfers between devices with their start and end apart: 4 -> 4, of which waited for: 1 -> 1; matrix products, arithmetic and copies ran while one was open for 13% -> 16% of each run, Pallas kernels for 0% -> 0%
where the time goes in v2:
time: 1710 us; the launch traced here: 1700 us
  Pallas kernels  1290 us (75%)
  matrix products  356 us (21%)
  local copies, waits for them, and re-layouts  18 us (1%)
    pallas_call x1, Pallas kernels, run_pipeline(): pl.pallas_call(functools.partial(pipeline_kernel, chunks, stages), in_spe...  1290 us
    dot_general x4, matrix products, dot_tn(): lax.dot_general(a, b, (((0,), (0,)), ((), ())), preferred_element_type=F32)  356 us
  transfers between devices with their start and end apart: 4, of which 1 were waited for; matrix products, arithmetic and copies ran while one was open for 16% of the time, Pallas kernels for 0%

profile of v2, /device:TPU:0, one launch (start us, length us, event | category | flops | bytes accessed | tf_op | source)
XLA Modules:
  0.0 1696.2 jit_solution(13172865077905857228)
XLA Ops:
  7.2 0.0 reduce-scatter.5.cloned.1.call-start
  7.2 4.6 copy.16.refs_2_
  11.8 1294.2 %pipeline.1 = (bf16[48,2,128,1024]{3,2,1,0:T(8,128)(2,1)}, bf16[48,256,1024]{2,1,0:T(8,128)(2,1)}, bf16[48,256,3072]{2,1,0:T(8,128)(2,1)}, bf16[48,256,1024]{2,1...) custom-call(bf16[48,2,128,1024]{3,2,1,0:T(8,128)(2,1)} %bitcast.30, ...), custom_call_target="tpu_custom_call" | custom-call | flops 618475290624 | bytes 1000000000 | tf_op jit(solution)/shard_map/pipeline/pallas_call | solution.py:379
  1306.0 88.9 %convolution_bitcast_fusion.1 = f32[1024,3072]{1,0:T(8,128)} fusion(bf16[48,256,1024]{2,1,0:T(8,128)(2,1)} %get-tuple-element.14, bf16[48,256,3072]{2,1,0:T(8,128)(2,1)} %get-tuple-element.15), kind=kOutput, calls=%fused_computation.1 | convolution fusion | flops 77309411328 | bytes 113246208 | tf_op jit(solution)/shard_map/dot_general | solution.py:35
  1394.9 0.0 reduce-scatter.5.cloned.1.call-update
  1394.9 0.0 reduce-scatter.7.cloned.1.call-start
  1395.0 33.0 %convolution_bitcast_fusion.2 = f32[1024,1024]{1,0:T(8,128)} fusion(bf16[48,256,1024]{2,1,0:T(8,128)(2,1)} %get-tuple-element.16, bf16[48,256,1024]{2,1,0:T(8,128)(2,1)} %get-tuple-element.17), kind=kOutput, calls=%fused_computation.2 | convolution fusion | flops 25769803776 | bytes 54525952 | tf_op jit(solution)/shard_map/dot_general | solution.py:35
  1428.0 0.0 reduce-scatter.7.cloned.1.call-update
  1428.0 0.0 reduce-scatter.9.cloned.1.call-start
  1428.1 117.1 %convolution_bitcast_fusion = f32[1024,4096]{1,0:T(8,128)} fusion(bf16[48,256,1024]{2,1,0:T(8,128)(2,1)} %get-tuple-element.18, bf16[48,256,4096]{2,1,0:T(8,128)(2,1)} %get-tuple-element.19), kind=kOutput, calls=%fused_computation | convolution fusion | flops 103079215104 | bytes 142606336 | tf_op jit(solution)/shard_map/dot_general | solution.py:35
  1545.2 0.0 reduce-scatter.9.cloned.1.call-update
  1545.2 0.0 reduce-scatter.11.cloned.1.call-start
  1545.3 116.6 %fusion = f32[4096,1024]{1,0:T(8,128)} fusion(bf16[12288,4096]{1,0:T(8,128)(2,1)} %bitcast.12, bf16[12288,1024]{1,0:T(8,128)(2,1)} %bitcast.38), kind=kOutput, calls=%fused_computation.3 | convolution fusion | flops 103079215104 | bytes 142606336 | tf_op jit(solution)/shard_map/dot_general | solution.py:35
  1661.9 0.0 reduce-scatter.11.cloned.1.call-update
  1661.9 0.0 reduce-scatter.5.cloned.1.call-done
  1661.9 6.6 copy.18
  1668.5 0.0 reduce-scatter.7.cloned.1.call-done
  1668.5 0.0 reduce-scatter.9.cloned.1.call-done
  1668.5 14.0 reduce-scatter.11.cloned.1.call-done
  1682.5 6.8 copy.25
Async XLA Ops:
  7.2 1654.8 %reduce-scatter.5.cloned.1.call-start = ((), (), s32[]{:S(2)}) async-start(), calls=%async_computation.4 | async-start | bytes 18874368 | tf_op jit(solution)/shard_map/reduce_scatter | solution.py:402
  1394.9 273.6 %reduce-scatter.7.cloned.1.call-start = ((), (), s32[]{:S(2)}) async-start(), calls=%async_computation.5 | async-start | bytes 6291456 | tf_op jit(solution)/shard_map/reduce_scatter | solution.py:402
  1428.0 240.5 %reduce-scatter.9.cloned.1.call-start = ((), (), s32[]{:S(2)}) async-start(), calls=%async_computation.6 | async-start | bytes 25165824 | tf_op jit(solution)/shard_map/reduce_scatter | solution.py:402
  1545.2 137.3 %reduce-scatter.11.cloned.1.call-start = ((), (), s32[]{:S(2)}) async-start(), calls=%async_computation.7 | async-start | bytes 25165824 | tf_op jit(solution)/shard_map/reduce_scatter | solution.py:402
Sparse Core Ops, SparseCore 0:
  1395.0 14.4 reduce-scatter.4
  1428.1 7.3 reduce-scatter.6
  1545.3 20.4 reduce-scatter.8
  1662.0 20.4 reduce-scatter.10
